TPU v7x, 256 devices: a whole 4x4x8 slice. The times are simulated.
256 devices in a mesh: row: 16 (over x_hi, z), col: 16 (over y, x_lo, core).
Axes of the slice: x: 4 (x_hi: 2, x_lo: 2; x = x_hi * 2 + x_lo), y: 4, z: 8, core: 2. Of those that a mesh axis runs over, the one named last changes fastest.
Arguments:
- tile_values: float32 [16, 16, 16, 128, 128], P('row', 'col'), may hold values from -0.1875 to 0.1875
- tile_rows: int32 [16, 16, 16], P('row', 'col'), may hold values from 0 to 15, as said below
- tile_cols: int32 [16, 16, 16], P('row', 'col'), may hold values from 0 to 63
- tile_live: int32 [16, 16, 16], P('row', 'col'), may hold values from 0 to 1, as said below
- dense_factor: float32 [512, 131072], P('row', 'col'), may hold values from -6 to 6
Outputs:
- product_transposed: float32 [512, 32768], P('col', 'row')
Inputs may be any that keep to these rules, and one draw needn't show every extreme that they name: `tile_rows`: tile row inside the block; the live tiles of one block have distinct (row, column) pairs. `tile_live`: in every block the live slots come first; the blocks (r, c) with |r − c| ≤ 1 have all 16 slots live; every other block has between 1 and 8 live slots.
All inputs are finite; a program needn't handle non-finite values.
Results may differ from a plain program's by a relative error of at most 0.0003.
Values sent between devices are 32-bit elements; how exact they have to be, the bound alone decides.
A program may use at most 64 MiB of HBM per device.

v0:
```python
import jax
import jax.numpy as jnp
from jax import lax
from jax.sharding import PartitionSpec as P

W = 512
RT = 16
CT = 64


def in_order(blocks, dim):
    blocks = jnp.moveaxis(blocks, 0, dim)
    shape = blocks.shape
    return blocks.reshape(*shape[:dim], shape[dim] * shape[dim + 1], *shape[dim + 2 :])


def from_everyone(value, axis):
    length = lax.axis_size(axis)
    return lax.all_to_all(
        jnp.broadcast_to(value[None], (length, *value.shape)), axis, 0, 0, tiled=True
    )


def gathered_copies(value, axis, dim):
    return in_order(from_everyone(value, axis), dim)


def in_blocks(value, dim, length):
    before, after = (value.shape[:dim], value.shape[dim + 1 :])
    return jnp.moveaxis(value.reshape(*before, length, -1, *after), dim, 0)


def sum_at_owner(value, axis, dim):
    length = lax.axis_size(axis)
    blocks = lax.all_to_all(in_blocks(value, dim, length), axis, 0, 0, tiled=True)
    return jnp.sum(blocks, axis=0)


def tile_product(selected, masked, onehot):
    product = jnp.einsum("wsk,sik->wsi", selected, masked, precision=lax.Precision.HIGHEST)
    placed = jnp.einsum("wsi,sr->wri", product, onehot, precision=lax.Precision.HIGHEST)
    return placed.reshape(selected.shape[0], onehot.shape[1] * selected.shape[2])


def body(tile_values, tile_rows, tile_cols, tile_live, dense_factor):
    blocks = tile_values[0, 0]
    row_ids = tile_rows[0, 0]
    slot_count = blocks.shape[0]
    tile_size = blocks.shape[1]
    width_share = dense_factor.shape[0]
    masked = blocks * tile_live[0, 0].astype(jnp.float32)[:, None, None]
    onehot = (row_ids[:, None] == jnp.arange(RT, dtype=jnp.int32)[None, :]).astype(jnp.float32)
    wanted = gathered_copies(tile_cols, "row", 0)
    wanted = wanted.reshape(lax.axis_size("row"), slot_count)
    outgoing = jnp.take(dense_factor.reshape(width_share, CT, tile_size), wanted, axis=1)
    incoming = lax.all_to_all(outgoing, "row", split_axis=1, concat_axis=0, tiled=True)
    partial_sum = tile_product(incoming.reshape(W, slot_count, tile_size), masked, onehot)
    return sum_at_owner(partial_sum, "col", 0)


def solution(mesh):
    in_specs = (
        P("row", "col", None, None, None),
        P("row", "col", None),
        P("row", "col", None),
        P("row", "col", None),
        P("row", "col"),
    )
    out_specs = P("col", "row")
    return jax.shard_map(body, mesh=mesh, in_specs=in_specs, out_specs=out_specs, check_vma=False)
```

profile of v0, /device:TPU:7, one launch (start us, length us, event | category | flops | bytes accessed | tf_op | source)
XLA Modules:
  0.0 215.4 jit_solution(13676004355256007897)
XLA Ops:
  0.0 0.0 copy-start
  0.0 1.3 broadcast_in_dim.21
  1.3 10.9 %all-to-all-start = ((s32[16,1,1,16]{3,2,1,0:T(1,128)}), s32[16,1,1,16]{3,2,1,0:T(1,128)S(1)}, u32[]{:S(2)}, u32[]{:S(2)}) async-start(s32[16,1,1,16]{3,2,1,0:T(1,128)} %broadcast_in_dim.21), calls=%async_computation | async-start | bytes 16384 | tf_op jit(solution)/shard_map/all_to_all | solution.py:19
  12.2 0.0 copy-done
  12.2 0.1 copy_bitcast_fusion
  12.4 6.1 %all-to-all-done = s32[16,1,1,16]{3,2,1,0:T(1,128)S(1)} async-done(((s32[16,1,1,16]{3,2,1,0:T(1,128)}), s32[16,1,1,16]{3,2,1,0:T(1,128)S(1)}, u32[]{:S(2)}, u32[]{:S(2)}) %all-to-all-start) | async-done | bytes 1056 | tf_op jit(solution)/shard_map/all_to_all | solution.py:19
  18.4 0.1 reshape.55
  18.5 3.0 %gather_fusion = f32[256,32,128]{2,1,0:T(8,128)} fusion(f32[32,64,128]{2,0,1:T(8,128)S(1)} %copy_bitcast_fusion, s32[1024]{0:T(1024)S(1)} %pad_clamp_fusion), kind=kCustom, calls=%fused_computation | custom fusion | bytes 8389632 | tf_op jit(solution)/shard_map/jit(_take)/gather | solution.py:55
  21.5 7.9 %fusion.2 = f32[32,16,16,128]{3,2,0,1:T(8,128)} fusion(f32[16,16,32,128]{3,2,1,0:T(8,128)} %bitcast.32, pred[16,16]{1,0:T(8,128)(4,1)S(1)} %compare_and_fusion), kind=kLoop, calls=%fused_computation.4 | loop fusion | flops 1048576 | bytes 8388864 | tf_op jit(solution)/shard_map/jit(_take)/select_n | solution.py:55
  29.4 0.0 copy-start.3
  29.4 0.0 copy-start.1
  29.4 7.1 %all-to-all-start.1 = ((f32[32,16,16,128]{3,2,0,1:T(8,128)}), f32[32,16,16,128]{3,2,0,1:T(8,128)}, u32[]{:S(2)}, u32[]{:S(2)}) async-start(f32[32,16,16,128]{3,2,0,1:T(8,128)} %fusion.2), calls=%async_computation.1 | async-start | bytes 8388608 | tf_op jit(solution)/shard_map/all_to_all | solution.py:56
  36.6 0.0 copy-done.3
  36.6 93.7 %all-to-all-done.1 = f32[32,16,16,128]{3,2,0,1:T(8,128)} async-done(((f32[32,16,16,128]{3,2,0,1:T(8,128)}), f32[32,16,16,128]{3,2,0,1:T(8,128)}, u32[]{:S(2)}, u32[]{:S(2)}) %all-to-all-start.1) | async-done | bytes 4194336 | tf_op jit(solution)/shard_map/all_to_all | solution.py:56
  130.3 0.0 copy-done.1
  130.3 9.4 %fusion.3 = f32[512,16,128]{0,2,1:T(8,128)} fusion(f32[512,16,128]{2,1,0:T(8,128)} %bitcast.11, f32[1,1,16,128,128]{4,3,2,1,0:T(8,128)S(1)} %copy-done.1, f32[16]{0:T(128)S(1)} %convert_bitcast_fusion), kind=kOutput, calls=%fused_computation.6 | convolution fusion | flops 1610874880 | bytes 9437248 | tf_op jit(solution)/shard_map/wsk,sik->wsi/dot_general | solution.py:40
  139.7 0.0 copy-start.2
  139.7 5.4 %copy.14 = f32[512,16,128]{2,1,0:T(8,128)} copy(f32[512,16,128]{0,2,1:T(8,128)} %fusion.3) | data formatting | bytes 8388608 | tf_op jit(solution)/shard_map/wsk,sik->wsi/transpose | solution.py:40
  145.1 0.0 copy-done.2
  145.1 6.2 %convolution_bitcast_fusion = f32[512,16,128]{2,1,0:T(8,128)} fusion(f32[512,16,128]{2,1,0:T(8,128)} %copy.14, s32[16]{0:T(128)S(1)} %bitcast.35), kind=kOutput, calls=%fused_computation.5 | convolution fusion | flops 201326848 | bytes 8388672 | tf_op jit(solution)/shard_map/wsi,sr->wri/dot_general | solution.py:41
  151.4 4.9 %reshape_reshape.10 = f32[16,32,2048]{2,1,0:T(8,128)} reshape(f32[512,16,128]{2,1,0:T(8,128)} %convolution_bitcast_fusion) | data formatting | bytes 8388608 | tf_op jit(solution)/shard_map/reshape;reshape | solution.py:30
  156.2 56.1 %all_to_all.25 = f32[16,32,2048]{2,1,0:T(8,128)} all-to-all(f32[16,32,2048]{2,1,0:T(8,128)} %reshape_reshape.10), channel_id=1, replica_groups=mesh['row'=16,'col'=16] {'col'}, dimensions={0} | all-to-all | bytes 8388608 | tf_op jit(solution)/shard_map/all_to_all | solution.py:35
  212.3 3.1 %reduce_sum.9 = f32[32,2048]{1,0:T(8,128)} reduce(f32[16,32,2048]{2,1,0:T(8,128)} %all_to_all.25, f32[]{:T(128)} %constant.17.clone.1), dimensions={0}, to_apply=%region_0.1 | reduce | flops 983040 | bytes 4456452 | tf_op jit(solution)/shard_map/reduce_sum | solution.py:36
  (4 shorter events, 0.0 us)
Async XLA Ops:
  0.0 12.2 %copy-start = (f32[32,8192]{1,0:T(8,128)S(1)}, f32[32,8192]{1,0:T(8,128)}, u32[]{:S(2)}) copy-start(f32[32,8192]{1,0:T(8,128)} %param.9) | copy-start | bytes 3145732
  1.3 17.1 %all-to-all-start = ((s32[16,1,1,16]{3,2,1,0:T(1,128)}), s32[16,1,1,16]{3,2,1,0:T(1,128)S(1)}, u32[]{:S(2)}, u32[]{:S(2)}) async-start(s32[16,1,1,16]{3,2,1,0:T(1,128)} %broadcast_in_dim.21), calls=%async_computation | async-start | bytes 16384 | tf_op jit(solution)/shard_map/all_to_all | solution.py:19
  29.4 7.1 %copy-start.3 = (s32[1,1,16]{2,1,0:T(1,128)S(1)}, s32[1,1,16]{2,1,0:T(1,128)}, u32[]{:S(2)}) copy-start(s32[1,1,16]{2,1,0:T(1,128)} %param.8) | copy-start | bytes 196
  29.4 100.8 %copy-start.1 = (f32[1,1,16,128,128]{4,3,2,1,0:T(8,128)S(1)}, f32[1,1,16,128,128]{4,3,2,1,0:T(8,128)}, u32[]{:S(2)}) copy-start(f32[1,1,16,128,128]{4,3,2,1,0:T(8,128)} %param.5) | copy-start | bytes 3145732
  29.4 100.8 %all-to-all-start.1 = ((f32[32,16,16,128]{3,2,0,1:T(8,128)}), f32[32,16,16,128]{3,2,0,1:T(8,128)}, u32[]{:S(2)}, u32[]{:S(2)}) async-start(f32[32,16,16,128]{3,2,0,1:T(8,128)} %fusion.2), calls=%async_computation.1 | async-start | bytes 8388608 | tf_op jit(solution)/shard_map/all_to_all | solution.py:56
  139.7 5.5 %copy-start.2 = (s32[1,1,16]{2,1,0:T(1,128)S(1)}, s32[1,1,16]{2,1,0:T(1,128)}, u32[]{:S(2)}) copy-start(s32[1,1,16]{2,1,0:T(1,128)} %param.6) | copy-start | bytes 196
where the time goes:
time: 218 us; the launch traced here: 215 us
  waiting for transfers between devices  99.8 us (46%)
  blocking collectives  56.1 us (26%)
  starting transfers between devices  18 us (8%)
  matrix products  15.7 us (7%)
  local copies, waits for them, and re-layouts  14.9 us (7%)
  other arithmetic  11.1 us (5%)
    all_to_all x1, waiting for transfers between devices, body(): lax.all_to_all(outgoing, 'row', split_axis=1, concat_axis=0, tiled=True)  93.7 us
    all_to_all x1, blocking collectives, sum_at_owner(): lax.all_to_all(in_blocks(value, dim, length), axis, 0, 0, tiled=True)  56.1 us
    all_to_all x1, starting transfers between devices, from_everyone(): lax.all_to_all(jnp.broadcast_to(value[None], (length, *value.shape)), axi...  10.9 us
    dot_general x1, matrix products, tile_product(): jnp.einsum('wsk,sik->wsi', selected, masked, precision=lax.Precision.HIGH...  9.41 us
    select_n x2, other arithmetic, body(): jnp.take(dense_factor.reshape(width_share, CT, tile_size), wanted, axis=1)  7.92 us
    all_to_all x1, starting transfers between devices, body(): lax.all_to_all(outgoing, 'row', split_axis=1, concat_axis=0, tiled=True)  7.11 us
    dot_general x1, matrix products, tile_product(): jnp.einsum('wsi,sr->wri', product, onehot, precision=lax.Precision.HIGHEST)  6.24 us
    all_to_all x1, waiting for transfers between devices, from_everyone(): lax.all_to_all(jnp.broadcast_to(value[None], (length, *value.shape)), axi...  6.05 us
  transfers between devices with their start and end apart: 2, of which 2 were waited for; matrix products, arithmetic and copies ran while one was open for 0% of the time, Pallas kernels for 0%

commit v1 on v0

v1 whole, which is shorter than its diff:
```python
import jax
import jax.numpy as jnp
from jax import lax
from jax.experimental import pallas as pl
from jax.experimental.pallas import tpu as pltpu
from jax.sharding import PartitionSpec as P

NX, NY, NZ = 4, 4, 8
TS = 128
SHARE = 32
RT = 16
CT = 64
SLOTS = 16
PER = 2
CHUNKS = SLOTS // PER
HALF = CHUNKS // 2
PIECES = 4
SPAN = CT * TS // (2 * PIECES)
MESH = pl.DeviceIdType.MESH


def rem(a, b):
    return lax.rem(a, jnp.int32(b))


def div(a, b):
    return lax.div(a, jnp.int32(b))


def kernel(
    tiles, listed, dense, out,
    held, lists, lists_s, relay, both, split, acc, near, far, pair, done,
    local_sem, right_send, right_recv, left_send, left_recv,
    hop1_send, hop1_recv, hop2_send, hop2_recv, list_send, list_recv,
    near_send, near_recv, far_send, far_recv, pair_send, pair_recv, out_send, out_recv,
):
    row, col = lax.axis_index("row"), lax.axis_index("col")
    x_hi, z = div(row, NZ), rem(row, NZ)
    y, x_lo, core = div(col, 4), rem(div(col, 2), 2), rem(col, 2)
    x = x_hi * 2 + x_lo

    def device(x, y, z, core):
        return (div(x, 2) * NZ + z, y * 4 + rem(x, 2) * 2 + core)

    def copy(src, dst, send_sem, recv_sem, target):
        return pltpu.make_async_remote_copy(
            src_ref=src, dst_ref=dst, send_sem=send_sem, recv_sem=recv_sem,
            device_id=target, device_id_type=MESH,
        )

    up = device(x, y, rem(z + 1, NZ), core)
    down = device(x, y, rem(z + NZ - 1, NZ), core)

    def banded(source):
        gap = x_hi * NZ + source - col
        return jnp.logical_and(gap >= -1, gap <= 1)

    def ring(level, j, rightwards):
        if rightwards:
            source = rem(z + NZ - level, NZ)
        else:
            source = rem(z + level, NZ)
        part = held.at[source, pl.ds(PER * j, PER)]
        return source, part

    def listed_part(source, j, level, rightwards):
        there = jnp.logical_or(j < HALF, banded(source))
        if level == 3:
            first = rem(j, HALF) < HALF // 2
            there = jnp.logical_and(there, first if rightwards else jnp.logical_not(first))
        return there

    def ring_copy(level, j, rightwards):
        source, part = ring(level, j, rightwards)
        if rightwards:
            made = copy(part, part, right_send.at[level, j], right_recv.at[level, j], up)
        else:
            made = copy(part, part, left_send.at[level, j], left_recv.at[level, j], down)
        return listed_part(source, j, level, rightwards), made

    def ring_arrival(level, j, rightwards):
        source, part = ring(level + 1, j, rightwards)
        if rightwards:
            made = copy(part, part, right_send.at[level, j], right_recv.at[level, j], up)
        else:
            made = copy(part, part, left_send.at[level, j], left_recv.at[level, j], down)
        return listed_part(source, j, level, rightwards), made

    def ring_start(level, j):
        for rightwards in (True, False):
            there, made = ring_copy(level, j, rightwards)
            pl.when(there)(made.start)

    def ring_wait(level, j):
        for rightwards in (True, False):
            there, made = ring_arrival(level, j, rightwards)
            pl.when(there)(made.wait_recv)

    forth = device(rem(x + 1, NX), y, z, core)
    back = device(rem(x + NX - 1, NX), y, z, core)

    def columns(way, k):
        return pl.ds(pl.multiple_of((way * PIECES + k) * SPAN, SPAN), SPAN)

    def hop1(way, k):
        return copy(
            both.at[x_hi, :, columns(way, k)], relay.at[way, k],
            hop1_send.at[way, k], hop1_recv.at[way, k], (forth, back)[way],
        )

    def hop2(way, k):
        origin = div(rem(x + (NX - 1 if way == 0 else 1), NX), 2)
        return copy(
            relay.at[way, k], both.at[origin, :, columns(way, k)],
            hop2_send.at[way, k], hop2_recv.at[way, k], (forth, back)[way],
        )

    def hop2_arrival(way, k):
        return copy(
            relay.at[way, k], both.at[1 - x_hi, :, columns(way, k)],
            hop2_send.at[way, k], hop2_recv.at[way, k], (forth, back)[way],
        )

    def list_copy(p):
        target = device(x, y, rem(z + p, NZ), core)
        return copy(lists.at[z], lists.at[z], list_send.at[p], list_recv.at[z], target)

    def list_arrival(p):
        source = rem(z + p, NZ)
        target = device(x, y, source, core)
        return copy(lists.at[source], lists.at[source], list_send.at[p], list_recv.at[source], target)

    own_dense = pltpu.make_async_copy(dense, both.at[x_hi], local_sem.at[0])
    own_tiles = pltpu.make_async_copy(tiles, held.at[z], local_sem.at[1])
    own_list = pltpu.make_async_copy(listed, lists.at[z], local_sem.at[2])
    own_list.start()
    own_tiles.start()
    own_dense.start()
    own_list.wait()

    @pl.loop(1, NZ)
    def _(p):
        list_copy(p).start()

    own_tiles.wait()

    @pl.loop(0, CHUNKS)
    def _(j):
        ring_start(0, j)

    own_dense.wait()

    @pl.loop(0, PIECES)
    def _(k):
        hop1(0, k).start()
        hop1(1, k).start()

    @pl.loop(0, NZ * RT)
    def _(i):
        acc[div(i, RT), rem(i, RT)] = jnp.zeros((2 * SHARE, TS), jnp.float32)

    def one_tile(b, slot):
        tile = held[b, slot]
        high = tile.astype(jnp.bfloat16)
        low = (tile - high.astype(jnp.float32)).astype(jnp.bfloat16)
        chosen = split[lists_s[b, 1, slot]]
        dims = (((1,), (1,)), ((), ()))
        by_high = lax.dot_general(chosen, high, dims, preferred_element_type=jnp.float32)
        by_low = lax.dot_general(
            chosen[: 2 * SHARE], low, dims, preferred_element_type=jnp.float32
        )
        return by_high[: 2 * SHARE] + (by_high[2 * SHARE :] + by_low)

    def multiply(b, j):
        @pl.when(jnp.logical_or(j < HALF, banded(b)))
        def _():
            products = [one_tile(b, PER * j + s) for s in range(PER)]
            for k in range(RT):
                term = acc[b, k]
                for s in range(PER):
                    slot = PER * j + s
                    live = lists_s[b, 2, slot].astype(jnp.float32)
                    weight = jnp.where(lists_s[b, 0, slot] == k, live, 0.0)
                    term = term + weight * products[s]
                acc[b, k] = term

    def near_copy(b):
        return copy(
            acc.at[b, pl.ds((1 - core) * 8, 8)], near.at[b],
            near_send.at[b], near_recv.at[b], device(x, y, z, 1 - core),
        )

    def far_copy(b, step):
        there = rem(y + step, NY)
        return copy(
            acc.at[b, pl.ds(core * 8 + there * 2, 2)], far.at[b, step - 1],
            far_send.at[b, step - 1], far_recv.at[b, step - 1], device(x, there, z, core),
        )

    def pair_copy(b):
        return copy(
            acc.at[b, core * 8 + y * 2 + (1 - x_lo)], pair.at[b],
            pair_send.at[b], pair_recv.at[b], device(x_hi * 2 + 1 - x_lo, y, z, core),
        )

    mine = core * 8 + y * 2 + x_lo

    def out_copy(b, a):
        return copy(
            done.at[b, pl.ds(a * SHARE, SHARE)], out.at[:, pl.ds(pl.multiple_of(mine * TS, TS), TS)],
            out_send.at[b, a], out_recv.at[mine], (x_hi * NZ + b, a * NZ + z),
        )

    def stage1(b):
        near_copy(b).start()

    def stage2(b):
        near_copy(b).wait_recv()

        @pl.loop(0, 8)
        def _(k):
            acc[b, core * 8 + k] = acc[b, core * 8 + k] + near[b, k]

        for step in (1, 2, 3):
            far_copy(b, step).start()

    def stage3(b):
        for step in (1, 2, 3):
            far_copy(b, step).wait_recv()
        for k in range(2):
            place = core * 8 + y * 2 + k
            acc[b, place] = acc[b, place] + (far[b, 0, k] + far[b, 1, k] + far[b, 2, k])
        pair_copy(b).start()

    def is_home(b, a):
        return jnp.logical_and(b == z, a * NZ + z == col)

    def stage4(b):
        pair_copy(b).wait_recv()
        done[b] = acc[b, mine] + pair[b]
        for a in range(2):
            home = is_home(b, a)

            @pl.when(home)
            def _():
                out[:, pl.ds(pl.multiple_of(mine * TS, TS), TS)] = done[b, a * SHARE : (a + 1) * SHARE]

            @pl.when(jnp.logical_not(home))
            def _():
                out_copy(b, a).start()

    @pl.loop(0, CHUNKS)
    def _(j):
        @pl.when(j < PIECES)
        def _():
            for way in (0, 1):
                hop1(way, j).wait_recv()
                hop2(way, j).start()

        ring_wait(0, j)
        ring_start(1, j)

    @pl.loop(0, CHUNKS)
    def _(j):
        ring_wait(1, j)
        ring_start(2, j)

    @pl.loop(1, NZ)
    def _(p):
        list_arrival(p).wait_recv()

    to_scalar = pltpu.make_async_copy(lists, lists_s, local_sem.at[3])
    to_scalar.start()

    @pl.loop(0, PIECES)
    def _(k):
        for way in (0, 1):
            hop2_arrival(way, k).wait_recv()

    @pl.loop(0, CT)
    def _(t):
        place = pl.ds(pl.multiple_of(t * TS, TS), TS)
        for a in range(2):
            value = both[a, :, place]
            high = value.astype(jnp.bfloat16)
            low = (value - high.astype(jnp.float32)).astype(jnp.bfloat16)
            split[t, a * SHARE : (a + 1) * SHARE] = high
            split[t, (2 + a) * SHARE : (3 + a) * SHARE] = low

    to_scalar.wait()

    def block(i):
        return rem(z + i + NZ, NZ)

    @pl.loop(0, CHUNKS)
    def _(j):
        ring_wait(2, j)
        ring_start(3, j)

        @pl.loop(0, 5)
        def _(i):
            multiply(block(i - 2), j)

    @pl.loop(0, 5)
    def _(i):
        stage1(block(i - 2))

    @pl.loop(0, CHUNKS)
    def _(j):
        for i in (-3, 3):
            multiply(block(i), j)

    stage1(block(-3))
    stage1(block(3))

    @pl.loop(0, 5)
    def _(i):
        stage2(block(i - 2))

    @pl.loop(0, CHUNKS)
    def _(j):
        ring_wait(3, j)
        multiply(block(4), j)

    stage1(block(4))

    @pl.loop(0, 5)
    def _(i):
        stage3(block(i - 2))

    stage2(block(-3))
    stage2(block(3))
    stage2(block(4))

    @pl.loop(0, 5)
    def _(i):
        stage4(block(i - 2))

    stage3(block(-3))
    stage3(block(3))
    stage3(block(4))
    stage4(block(-3))
    stage4(block(3))
    stage4(block(4))

    @pl.loop(0, RT)
    def _(t):
        source = (div(rem(t, 8), 2) * 2 + rem(t, 2)) * 2 + div(t, 8)
        there = out.at[:, pl.ds(pl.multiple_of(t * TS, TS), TS)]
        home = jnp.logical_and(source == col, rem(col, NZ) == z)

        @pl.when(jnp.logical_not(home))
        def _():
            copy(
                done.at[0, pl.ds(0, SHARE)], there, out_send.at[0, 0], out_recv.at[t],
                (row, rem(col + 1, 16)),
            ).wait_recv()

    @pl.loop(1, NZ)
    def _(p):
        list_copy(p).wait_send()

    @pl.loop(0, CHUNKS)
    def _(j):
        for level in range(4):
            for rightwards in (True, False):
                there, made = ring_copy(level, j, rightwards)
                pl.when(there)(made.wait_send)

    @pl.loop(0, PIECES)
    def _(k):
        for way in (0, 1):
            hop1(way, k).wait_send()
            hop2(way, k).wait_send()

    @pl.loop(0, NZ)
    def _(b):
        near_copy(b).wait_send()
        for step in (1, 2, 3):
            far_copy(b, step).wait_send()
        pair_copy(b).wait_send()
        for a in range(2):
            pl.when(jnp.logical_not(is_home(b, a)))(out_copy(b, a).wait_send)


def body(tile_values, tile_rows, tile_cols, tile_live, dense_factor):
    lists = jnp.concatenate(
        [tile_rows[0], tile_cols[0], tile_live[0], jnp.zeros((5, SLOTS), jnp.int32)], axis=0
    )
    lists = jnp.pad(lists, ((0, 0), (0, TS - SLOTS)))
    dma = pltpu.SemaphoreType.DMA
    vmem = pltpu.VMEM
    f32 = jnp.float32
    return pl.pallas_call(
        kernel,
        out_shape=jax.ShapeDtypeStruct((SHARE, RT * TS), f32),
        in_specs=[pl.BlockSpec(memory_space=pl.ANY)] * 3,
        out_specs=pl.BlockSpec(memory_space=pltpu.VMEM),
        scratch_shapes=[
            vmem((NZ, SLOTS, TS, TS), f32),
            vmem((NZ, 8, TS), jnp.int32),
            pltpu.SMEM((NZ, 8, TS), jnp.int32),
            vmem((2, PIECES, SHARE, SPAN), f32),
            vmem((2, SHARE, CT * TS), f32),
            vmem((CT, 4 * SHARE, TS), jnp.bfloat16),
            vmem((NZ, RT, 2 * SHARE, TS), f32),
            vmem((NZ, 8, 2 * SHARE, TS), f32),
            vmem((NZ, 3, 2, 2 * SHARE, TS), f32),
            vmem((NZ, 2 * SHARE, TS), f32),
            vmem((NZ, 2 * SHARE, TS), f32),
            dma((4,)),
            dma((4, CHUNKS)), dma((4, CHUNKS)), dma((4, CHUNKS)), dma((4, CHUNKS)),
            dma((2, PIECES)), dma((2, PIECES)), dma((2, PIECES)), dma((2, PIECES)),
            dma((NZ,)), dma((NZ,)),
            dma((NZ,)), dma((NZ,)), dma((NZ, 3)), dma((NZ, 3)), dma((NZ,)), dma((NZ,)),
            dma((NZ, 2)), dma((RT,)),
        ],
        compiler_params=pltpu.CompilerParams(
            has_side_effects=True, vmem_limit_bytes=48 * 1024 * 1024
        ),
    )(tile_values[0, 0], lists, dense_factor)


def solution(mesh):
    in_specs = (
        P("row", "col", None, None, None),
        P("row", "col", None),
        P("row", "col", None),
        P("row", "col", None),
        P("row", "col"),
    )
    out_specs = P("col", "row")
    return jax.shard_map(body, mesh=mesh, in_specs=in_specs, out_specs=out_specs, check_vma=False)
```

time: 218 us -> 132 us (0.61)
  the two profiles are of different devices: /device:TPU:7 before, /device:TPU:12 now
where the time goes in v1:
time: 132 us
  Pallas kernels  128 us (97%)
  local copies, waits for them, and re-layouts  3.84 us (3%)
    pallas_call x1, Pallas kernels, body(): pl.pallas_call(kernel, out_shape=jax.ShapeDtypeStruct((SHARE, RT * TS), f...  128 us
    unnamed x11, local copies, waits for them, and re-layouts  3.75 us

profile of v1, /device:TPU:12, one launch (start us, length us, event | category | flops | bytes accessed | tf_op | source)
XLA Modules:
  0.0 131.7 jit_solution(7223859099787663676)
XLA Ops:
  0.0 0.0 copy-start.2
  0.0 0.0 copy-start.3
  0.0 0.0 copy-start.4
  0.0 0.1 pad.8.clone
  0.1 0.6 copy-done.2
  0.7 0.0 copy-done.3
  0.7 0.0 copy-done.4
  0.7 0.1 add_add_fusion
  0.8 0.0 copy-start
  0.8 1.2 copy-done
  2.0 0.0 copy-start.1
  2.0 1.2 copy-done.1
  3.2 127.8 %shard_map.55 = f32[32,2048]{1,0:T(8,128)S(1)} custom-call(f32[16,128,128]{2,1,0:T(8,128)S(1)} %bitcast.4, s32[8,128]{1,0:T(8,128)S(1)} %pad.4.listed, f32[32,8192]{1,0:T(8,128)S(1)} %copy-done.1), custom_call_target="tpu_custom_call" | custom-call | tf_op jit(solution)/shard_map/pallas_call | solution.py:394
  131.0 0.7 copy.7
  (2 shorter events, 0.0 us)
Async XLA Ops:
  0.0 0.7 copy-start.2
  0.0 0.7 copy-start.3
  0.0 0.7 copy-start.4
  0.8 1.2 copy-start
  2.0 1.2 copy-start.1

commit v2 on v1

v2 whole, which is shorter than its diff:
```python
import jax
import jax.numpy as jnp
from jax import lax
from jax.experimental import pallas as pl
from jax.experimental.pallas import tpu as pltpu
from jax.sharding import PartitionSpec as P

NX, NY, NZ = 4, 4, 8
TS = 128
SHARE = 32
RT = 16
CT = 64
SLOTS = 16
PER = 2
CHUNKS = SLOTS // PER
HALF = CHUNKS // 2
PIECES = 4
SPAN = CT * TS // (2 * PIECES)
MESH = pl.DeviceIdType.MESH


def rem(a, b):
    return lax.rem(a, jnp.int32(b))


def div(a, b):
    return lax.div(a, jnp.int32(b))


def kernel(
    tiles, rows_in, cols_in, live_in, dense, out,
    held, lists, lists_s, relay, both, split, acc, near, far, pair, done,
    local_sem, tile_sem, dense_sem,
    right_send, right_recv, left_send, left_recv, list_send, list_recv,
    hop1_send, hop1_recv, hop2_send, hop2_recv,
    near_send, near_recv, far_send, far_recv, pair_send, pair_recv, out_send, out_recv,
):
    row, col = lax.axis_index("row"), lax.axis_index("col")
    x_hi, z = div(row, NZ), rem(row, NZ)
    y, x_lo, core = div(col, 4), rem(div(col, 2), 2), rem(col, 2)
    x = x_hi * 2 + x_lo

    def device(x, y, z, core):
        return (div(x, 2) * NZ + z, y * 4 + rem(x, 2) * 2 + core)

    def copy(src, dst, send_sem, recv_sem, target):
        return pltpu.make_async_remote_copy(
            src_ref=src, dst_ref=dst, send_sem=send_sem, recv_sem=recv_sem,
            device_id=target, device_id_type=MESH,
        )

    up = device(x, y, rem(z + 1, NZ), core)
    down = device(x, y, rem(z + NZ - 1, NZ), core)
    forth = device(rem(x + 1, NX), y, z, core)
    back = device(rem(x + NX - 1, NX), y, z, core)

    barrier = pltpu.get_barrier_semaphore()
    partners = [up, down, forth, back, device(x, y, z, 1 - core)]
    partners += [device(x, rem(y + step, NY), z, core) for step in (1, 2, 3)]
    for partner in partners:
        pl.semaphore_signal(barrier, inc=1, device_id=partner, device_id_type=MESH)

    center = col - x_hi * NZ

    def banded(source):
        gap = source - center
        return jnp.logical_and(gap >= -1, gap <= 1)

    def right_hops(source, j):
        u = rem(source - center + 3 + 4 * NZ, NZ) - 3
        second = j >= HALF
        first_hops = jnp.where(u > 0, 4, 3)
        second_hops = jnp.where(u < 0, 2, jnp.where(u > 0, 5, 4))
        even_hops = jnp.where(rem(j, HALF) < HALF // 2, 4, 3)
        crossed = jnp.logical_and(center >= -1, center <= NZ)
        return jnp.where(crossed, jnp.where(second, second_hops, first_hops), even_hops)

    def ring_message(level, source, j, rightwards):
        there = jnp.logical_or(j < HALF, banded(source))
        hops = right_hops(source, j)
        if not rightwards:
            hops = NZ - 1 - hops
        there = jnp.logical_and(there, level < hops)
        part = held.at[source, pl.ds(PER * j, PER)]
        if rightwards:
            return there, copy(part, part, right_send.at[level, j], right_recv.at[level, j], up)
        return there, copy(part, part, left_send.at[level, j], left_recv.at[level, j], down)

    def around(distance, rightwards):
        return rem(z + NZ - distance, NZ) if rightwards else rem(z + distance, NZ)

    def ring_start(level, j):
        for way in (True, False):
            there, made = ring_message(level, around(level, way), j, way)
            pl.when(there)(made.start)

    def ring_wait(level, j):
        for way in (True, False):
            there, made = ring_message(level, around(level + 1, way), j, way)
            pl.when(there)(made.wait_recv)

    def ring_sent(level, j):
        for way in (True, False):
            there, made = ring_message(level, around(level, way), j, way)
            pl.when(there)(made.wait_send)

    def list_message(level, distance, rightwards):
        part = lists.at[around(distance, rightwards)]
        way = 0 if rightwards else 1
        return copy(
            part, part, list_send.at[way, level], list_recv.at[way, level],
            up if rightwards else down,
        )

    def list_start(level):
        for way in (True, False)[: 2 if level < 3 else 1]:
            list_message(level, level, way).start()

    def list_wait(level):
        for way in (True, False)[: 2 if level < 3 else 1]:
            list_message(level, level + 1, way).wait_recv()

    def columns(way, k):
        return pl.ds(pl.multiple_of((way * PIECES + k) * SPAN, SPAN), SPAN)

    def hop1(way, k):
        return copy(
            both.at[x_hi, :, columns(way, k)], relay.at[way, k],
            hop1_send.at[way, k], hop1_recv.at[way, k], (forth, back)[way],
        )

    def hop2(way, k, owner):
        return copy(
            relay.at[way, k], both.at[owner, :, columns(way, k)],
            hop2_send.at[way, k], hop2_recv.at[way, k], (forth, back)[way],
        )

    def relayed(way):
        return div(rem(x + (NX - 1 if way == 0 else 1), NX), 2)

    own_lists = [
        pltpu.make_async_copy(ref, lists.at[z, k], local_sem.at[k])
        for k, ref in enumerate((rows_in, cols_in, live_in))
    ]

    def own_tiles(j):
        part = pl.ds(PER * j, PER)
        return pltpu.make_async_copy(tiles.at[part], held.at[z, part], tile_sem.at[j])

    def own_dense(way, k):
        part = columns(way, k)
        return pltpu.make_async_copy(
            dense.at[:, part], both.at[x_hi, :, part], dense_sem.at[way, k]
        )

    for made in own_lists:
        made.start()

    @pl.loop(0, CHUNKS)
    def _(j):
        own_tiles(j).start()

    @pl.loop(0, PIECES)
    def _(k):
        for way in (0, 1):
            own_dense(way, k).start()

    for made in own_lists:
        made.wait()
    pl.semaphore_wait(barrier, len(partners))
    list_start(0)

    @pl.loop(0, CHUNKS)
    def _(j):
        own_tiles(j).wait()
        ring_start(0, j)

        @pl.when(j < PIECES)
        def _():
            for way in (0, 1):
                own_dense(way, j).wait()
                hop1(way, j).start()

    @pl.loop(0, NZ * RT)
    def _(i):
        acc[div(i, RT), rem(i, RT)] = jnp.zeros((2 * SHARE, TS), jnp.float32)

    def one_tile(b, slot):
        tile = held[b, slot]
        high = tile.astype(jnp.bfloat16)
        low = (tile - high.astype(jnp.float32)).astype(jnp.bfloat16)
        chosen = split[lists_s[b, 1, 0, slot]]
        dims = (((1,), (1,)), ((), ()))
        by_high = lax.dot_general(chosen, high, dims, preferred_element_type=jnp.float32)
        by_low = lax.dot_general(
            chosen[: 2 * SHARE], low, dims, preferred_element_type=jnp.float32
        )
        return by_high[: 2 * SHARE] + (by_high[2 * SHARE :] + by_low)

    def multiply(b, j):
        @pl.when(jnp.logical_or(j < HALF, banded(b)))
        def _():
            products = [one_tile(b, PER * j + s) for s in range(PER)]
            for k in range(RT):
                term = acc[b, k]
                for s in range(PER):
                    slot = PER * j + s
                    live = lists_s[b, 2, 0, slot].astype(jnp.float32)
                    weight = jnp.where(lists_s[b, 0, 0, slot] == k, live, 0.0)
                    term = term + weight * products[s]
                acc[b, k] = term

    def near_copy(b):
        return copy(
            acc.at[b, pl.ds((1 - core) * 8, 8)], near.at[b],
            near_send.at[b], near_recv.at[b], device(x, y, z, 1 - core),
        )

    def far_copy(b, step):
        there = rem(y + step, NY)
        return copy(
            acc.at[b, pl.ds(core * 8 + there * 2, 2)], far.at[b, step - 1],
            far_send.at[b, step - 1], far_recv.at[b, step - 1], device(x, there, z, core),
        )

    def pair_copy(b):
        return copy(
            acc.at[b, core * 8 + y * 2 + (1 - x_lo)], pair.at[b],
            pair_send.at[b], pair_recv.at[b], device(x_hi * 2 + 1 - x_lo, y, z, core),
        )

    mine = core * 8 + y * 2 + x_lo

    def out_copy(b, a):
        return copy(
            done.at[b, pl.ds(a * SHARE, SHARE)], out.at[:, pl.ds(pl.multiple_of(mine * TS, TS), TS)],
            out_send.at[b, a], out_recv.at[mine], (x_hi * NZ + b, a * NZ + z),
        )

    def block(i):
        return rem(z + i + NZ, NZ)

    def stage1(i):
        near_copy(block(i)).start()

    def stage2(i):
        b = block(i)
        near_copy(b).wait_recv()

        @pl.loop(0, 8)
        def _(k):
            acc[b, core * 8 + k] = acc[b, core * 8 + k] + near[b, k]

        for step in (1, 2, 3):
            far_copy(b, step).start()

    def stage3(i):
        b = block(i)
        for step in (1, 2, 3):
            far_copy(b, step).wait_recv()
        for k in range(2):
            place = core * 8 + y * 2 + k
            acc[b, place] = acc[b, place] + (far[b, 0, k] + far[b, 1, k] + far[b, 2, k])
        pair_copy(b).start()

    def is_home(b, a):
        return jnp.logical_and(b == z, a * NZ + z == col)

    def stage4(i):
        b = block(i)
        pair_copy(b).wait_recv()
        done[b] = acc[b, mine] + pair[b]
        for a in range(2):
            home = is_home(b, a)

            @pl.when(home)
            def _():
                out[:, pl.ds(pl.multiple_of(mine * TS, TS), TS)] = done[b, a * SHARE : (a + 1) * SHARE]

            @pl.when(jnp.logical_not(home))
            def _():
                out_copy(b, a).start()

    @pl.loop(0, CHUNKS)
    def _(j):
        @pl.when(j < PIECES)
        def _():
            for way in (0, 1):
                hop1(way, j).wait_recv()
                hop2(way, j, relayed(way)).start()

        ring_wait(0, j)
        ring_start(1, j)
        for level in range(4):
            @pl.when(j == level)
            def _():
                list_wait(level)
                if level < 3:
                    list_start(level + 1)

    @pl.loop(0, HALF)
    def _(j):
        ring_wait(1, j)
        ring_start(2, j)

    to_scalar = pltpu.make_async_copy(lists, lists_s, local_sem.at[0])
    to_scalar.start()

    @pl.loop(0, PIECES)
    def _(k):
        for way in (0, 1):
            hop2(way, k, 1 - x_hi).wait_recv()

    @pl.loop(0, CT)
    def _(t):
        place = pl.ds(pl.multiple_of(t * TS, TS), TS)
        for a in range(2):
            value = both[a, :, place]
            high = value.astype(jnp.bfloat16)
            low = (value - high.astype(jnp.float32)).astype(jnp.bfloat16)
            split[t, a * SHARE : (a + 1) * SHARE] = high
            split[t, (2 + a) * SHARE : (3 + a) * SHARE] = low

    to_scalar.wait()

    @pl.loop(HALF, CHUNKS)
    def _(j):
        ring_wait(1, j)
        ring_start(2, j)

        @pl.loop(0, 3)
        def _(i):
            multiply(block(i - 1), j - HALF)
            multiply(block(i - 1), j)

    stage1(0)
    stage1(1)
    stage1(-1)

    @pl.loop(0, CHUNKS)
    def _(j):
        ring_wait(2, j)
        ring_start(3, j)
        multiply(block(2), j)
        multiply(block(-2), j)
        for i, when in ((0, 0), (1, 1), (-1, 2)):
            pl.when(j == when)(lambda i=i: stage2(i))

    stage1(2)
    stage1(-2)

    @pl.loop(0, CHUNKS)
    def _(j):
        ring_wait(3, j)
        ring_start(4, j)
        multiply(block(4), j)

        @pl.when(j < HALF)
        def _():
            multiply(block(3), j)
            multiply(block(-3), j)

        for i, when in ((2, 0), (-2, 1)):
            pl.when(j == when)(lambda i=i: stage2(i))
        for i, when in ((0, 2), (1, 3), (-1, 3)):
            pl.when(j == when)(lambda i=i: stage3(i))

    stage1(4)

    @pl.loop(HALF, CHUNKS)
    def _(j):
        ring_wait(4, j)
        multiply(block(3), j)
        multiply(block(-3), j)

    stage1(3)
    stage1(-3)
    for i in (0, 1, -1):
        stage4(i)
    stage2(4)
    stage3(2)
    stage3(-2)
    stage2(3)
    stage2(-3)
    stage4(2)
    stage4(-2)
    stage3(4)
    stage3(3)
    stage3(-3)
    stage4(4)
    stage4(3)
    stage4(-3)

    @pl.loop(0, RT)
    def _(t):
        source = (div(rem(t, 8), 2) * 2 + rem(t, 2)) * 2 + div(t, 8)
        there = out.at[:, pl.ds(pl.multiple_of(t * TS, TS), TS)]
        home = jnp.logical_and(source == col, rem(col, NZ) == z)

        @pl.when(jnp.logical_not(home))
        def _():
            copy(
                done.at[0, pl.ds(0, SHARE)], there, out_send.at[0, 0], out_recv.at[t],
                (row, rem(col + 1, 16)),
            ).wait_recv()

    for level in range(4):
        for way in (True, False)[: 2 if level < 3 else 1]:
            list_message(level, level, way).wait_send()

    @pl.loop(0, CHUNKS)
    def _(j):
        for level in range(5):
            ring_sent(level, j)

    @pl.loop(0, PIECES)
    def _(k):
        for way in (0, 1):
            hop1(way, k).wait_send()
            hop2(way, k, relayed(way)).wait_send()

    @pl.loop(0, NZ)
    def _(b):
        near_copy(b).wait_send()
        for step in (1, 2, 3):
            far_copy(b, step).wait_send()
        pair_copy(b).wait_send()
        for a in range(2):
            pl.when(jnp.logical_not(is_home(b, a)))(out_copy(b, a).wait_send)


def body(tile_values, tile_rows, tile_cols, tile_live, dense_factor):
    dma = pltpu.SemaphoreType.DMA
    vmem = pltpu.VMEM
    f32 = jnp.float32
    return pl.pallas_call(
        kernel,
        out_shape=jax.ShapeDtypeStruct((SHARE, RT * TS), f32),
        in_specs=[pl.BlockSpec(memory_space=pltpu.HBM)] * 5,
        out_specs=pl.BlockSpec(memory_space=pltpu.VMEM),
        scratch_shapes=[
            vmem((NZ, SLOTS, TS, TS), f32),
            vmem((NZ, 3, 1, SLOTS), jnp.int32),
            pltpu.SMEM((NZ, 3, 1, SLOTS), jnp.int32),
            vmem((2, PIECES, SHARE, SPAN), f32),
            vmem((2, SHARE, CT * TS), f32),
            vmem((CT, 4 * SHARE, TS), jnp.bfloat16),
            vmem((NZ, RT, 2 * SHARE, TS), f32),
            vmem((NZ, 8, 2 * SHARE, TS), f32),
            vmem((NZ, 3, 2, 2 * SHARE, TS), f32),
            vmem((NZ, 2 * SHARE, TS), f32),
            vmem((NZ, 2 * SHARE, TS), f32),
            dma((3,)), dma((CHUNKS,)), dma((2, PIECES)),
            dma((5, CHUNKS)), dma((5, CHUNKS)), dma((5, CHUNKS)), dma((5, CHUNKS)),
            dma((2, 4)), dma((2, 4)),
            dma((2, PIECES)), dma((2, PIECES)), dma((2, PIECES)), dma((2, PIECES)),
            dma((NZ,)), dma((NZ,)), dma((NZ, 3)), dma((NZ, 3)), dma((NZ,)), dma((NZ,)),
            dma((NZ, 2)), dma((RT,)),
        ],
        compiler_params=pltpu.CompilerParams(
            collective_id=0, has_side_effects=True, vmem_limit_bytes=48 * 1024 * 1024
        ),
    )(tile_values[0, 0], tile_rows[0], tile_cols[0], tile_live[0], dense_factor)


def solution(mesh):
    in_specs = (
        P("row", "col", None, None, None),
        P("row", "col", None),
        P("row", "col", None),
        P("row", "col", None),
        P("row", "col"),
    )
    out_specs = P("col", "row")
    return jax.shard_map(body, mesh=mesh, in_specs=in_specs, out_specs=out_specs, check_vma=False)
```

time: 132 us -> 113 us (0.86)
  the two profiles are of different devices: /device:TPU:12 before, /device:TPU:40 now
where the time goes in v2:
time: 113 us
  Pallas kernels  109 us (96%)
  local copies, waits for them, and re-layouts  3.84 us (3%)
    pallas_call x1, Pallas kernels, body(): pl.pallas_call(kernel, out_shape=jax.ShapeDtypeStruct((SHARE, RT * TS), f...  109 us
    unnamed x11, local copies, waits for them, and re-layouts  3.84 us

profile of v2, /device:TPU:40, one launch (start us, length us, event | category | flops | bytes accessed | tf_op | source)
XLA Modules:
  0.0 113.3 jit_solution(16599633338035921091)
XLA Ops:
  0.0 0.0 copy-start.2
  0.0 0.0 copy-start.3
  0.0 0.0 copy-start.4
  0.0 0.6 copy-done.2
  0.7 0.0 copy-done.3
  0.7 0.0 copy-done.4
  0.7 0.0 copy-start
  0.7 1.2 %copy-done = f32[1,1,16,128,128]{4,3,2,1,0:T(8,128)S(1)} copy-done((f32[1,1,16,128,128]{4,3,2,1,0:T(8,128)S(1)}, f32[1,1,16,128,128]{4,3,2,1,0:T(8,128)}, u32[]{:S(2)}) %copy-start) | copy-done | bytes 1048600
  1.9 0.0 copy-start.1
  1.9 1.2 %copy-done.1 = f32[32,8192]{1,0:T(8,128)S(1)} copy-done((f32[32,8192]{1,0:T(8,128)S(1)}, f32[32,8192]{1,0:T(8,128)}, u32[]{:S(2)}) %copy-start.1) | copy-done | bytes 1048600
  3.1 109.5 %shard_map.55 = f32[32,2048]{1,0:T(8,128)S(1)} custom-call(f32[16,128,128]{2,1,0:T(8,128)S(1)} %bitcast.4, s32[1,16]{1,0:T(1,128)S(1)} %bitcast.5, s32[1,16]{1,0:T(1,128)S(1)} %bitcast.6, s32[1,16]{1,0:T(1,128)S(1)} %bitcast.7, f32[32,8192]{1,0:T(8,128)S(1)} %copy-done.1), custom_call_target="tpu_custom_call" | custom-call | tf_op jit(solution)/shard_map/pallas_call | solution.py:436
  112.6 0.7 copy.7
Async XLA Ops:
  0.0 0.7 copy-start.2
  0.0 0.7 copy-start.3
  0.0 0.7 copy-start.4
  0.7 1.2 %copy-start = (f32[1,1,16,128,128]{4,3,2,1,0:T(8,128)S(1)}, f32[1,1,16,128,128]{4,3,2,1,0:T(8,128)}, u32[]{:S(2)}) copy-start(f32[1,1,16,128,128]{4,3,2,1,0:T(8,128)} %param.5) | copy-start | bytes 3145732
  1.9 1.2 %copy-start.1 = (f32[32,8192]{1,0:T(8,128)S(1)}, f32[32,8192]{1,0:T(8,128)}, u32[]{:S(2)}) copy-start(f32[32,8192]{1,0:T(8,128)} %dense.1) | copy-start | bytes 3145732

commit v3 on v2

--- a/solution.py
+++ b/solution.py
@@ -55,7 +55,8 @@
     back = device(rem(x + NX - 1, NX), y, z, core)
 
     barrier = pltpu.get_barrier_semaphore()
-    partners = [up, down, forth, back, device(x, y, z, 1 - core)]
+    partners = [device(x, y, rem(z + step, NZ), core) for step in range(1, NZ)]
+    partners += [forth, back, device(x, y, z, 1 - core)]
     partners += [device(x, rem(y + step, NY), z, core) for step in (1, 2, 3)]
     for partner in partners:
         pl.semaphore_signal(barrier, inc=1, device_id=partner, device_id_type=MESH)
@@ -104,21 +105,18 @@
             there, made = ring_message(level, around(level, way), j, way)
             pl.when(there)(made.wait_send)
 
-    def list_message(level, distance, rightwards):
-        part = lists.at[around(distance, rightwards)]
-        way = 0 if rightwards else 1
-        return copy(
-            part, part, list_send.at[way, level], list_recv.at[way, level],
-            up if rightwards else down,
-        )
-
-    def list_start(level):
-        for way in (True, False)[: 2 if level < 3 else 1]:
-            list_message(level, level, way).start()
-
-    def list_wait(level):
-        for way in (True, False)[: 2 if level < 3 else 1]:
-            list_message(level, level + 1, way).wait_recv()
+    def list_copy(p):
+        peer = rem(z + p, NZ)
+        return copy(
+            lists.at[z], lists.at[z], list_send.at[p], list_recv.at[z], device(x, y, peer, core)
+        )
+
+    def list_arrival(p):
+        peer = rem(z + p, NZ)
+        return copy(
+            lists.at[peer], lists.at[peer], list_send.at[p], list_recv.at[peer],
+            device(x, y, peer, core),
+        )
 
     def columns(way, k):
         return pl.ds(pl.multiple_of((way * PIECES + k) * SPAN, SPAN), SPAN)
@@ -168,7 +166,10 @@
     for made in own_lists:
         made.wait()
     pl.semaphore_wait(barrier, len(partners))
-    list_start(0)
+
+    @pl.loop(1, NZ)
+    def _(p):
+        list_copy(p).start()
 
     @pl.loop(0, CHUNKS)
     def _(j):
@@ -291,17 +292,15 @@
 
         ring_wait(0, j)
         ring_start(1, j)
-        for level in range(4):
-            @pl.when(j == level)
-            def _():
-                list_wait(level)
-                if level < 3:
-                    list_start(level + 1)
 
     @pl.loop(0, HALF)
     def _(j):
         ring_wait(1, j)
         ring_start(2, j)
+
+    @pl.loop(1, NZ)
+    def _(p):
+        list_arrival(p).wait_recv()
 
     to_scalar = pltpu.make_async_copy(lists, lists_s, local_sem.at[0])
     to_scalar.start()
@@ -404,9 +403,9 @@
                 (row, rem(col + 1, 16)),
             ).wait_recv()
 
-    for level in range(4):
-        for way in (True, False)[: 2 if level < 3 else 1]:
-            list_message(level, level, way).wait_send()
+    @pl.loop(1, NZ)
+    def _(p):
+        list_copy(p).wait_send()
 
     @pl.loop(0, CHUNKS)
     def _(j):
@@ -452,13 +451,13 @@
             vmem((NZ, 2 * SHARE, TS), f32),
             dma((3,)), dma((CHUNKS,)), dma((2, PIECES)),
             dma((5, CHUNKS)), dma((5, CHUNKS)), dma((5, CHUNKS)), dma((5, CHUNKS)),
-            dma((2, 4)), dma((2, 4)),
+            dma((NZ,)), dma((NZ,)),
             dma((2, PIECES)), dma((2, PIECES)), dma((2, PIECES)), dma((2, PIECES)),
             dma((NZ,)), dma((NZ,)), dma((NZ, 3)), dma((NZ, 3)), dma((NZ,)), dma((NZ,)),
             dma((NZ, 2)), dma((RT,)),
         ],
         compiler_params=pltpu.CompilerParams(
-            collective_id=0, has_side_effects=True, vmem_limit_bytes=48 * 1024 * 1024
+            collective_id=0, has_side_effects=True, vmem_limit_bytes=67043328
         ),
     )(tile_values[0, 0], tile_rows[0], tile_cols[0], tile_live[0], dense_factor)
 

time: 113 us -> 105 us (0.929)
  the two profiles are of different devices: /device:TPU:40 before, /device:TPU:7 now
where the time goes in v3:
time: 105 us
  Pallas kernels  103 us (98%)
  local copies, waits for them, and re-layouts  1.67 us (2%)
    pallas_call x1, Pallas kernels, body(): pl.pallas_call(kernel, out_shape=jax.ShapeDtypeStruct((SHARE, RT * TS), f...  103 us

profile of v3, /device:TPU:7, one launch (start us, length us, event | category | flops | bytes accessed | tf_op | source)
XLA Modules:
  0.0 105.1 jit_solution(12312468847657497053)
XLA Ops:
  0.0 103.4 %shard_map.55 = f32[32,2048]{1,0:T(8,128)} custom-call(f32[16,128,128]{2,1,0:T(8,128)} %bitcast.4, s32[1,16]{1,0:T(1,128)} %bitcast.5, s32[1,16]{1,0:T(1,128)} %bitcast.6, s32[1,16]{1,0:T(1,128)} %bitcast.7, f32[32,8192]{1,0:T(8,128)} %dense.1), custom_call_target="tpu_custom_call" | custom-call | tf_op jit(solution)/shard_map/pallas_call | solution.py:435
  103.5 1.7 %copy.7 = f32[32,2048]{1,0:T(8,128)} copy(f32[32,2048]{1,0:T(8,128)} %shard_map.55) | data formatting | bytes 524288

commit v4 on v0

v4 whole, which is shorter than its diff:
```python
import jax
import jax.numpy as jnp
from jax import lax
from jax.experimental import pallas as pl
from jax.experimental.pallas import tpu as pltpu
from jax.sharding import PartitionSpec as P

NX, NY, NZ = 4, 4, 8
TS = 128
SHARE = 32
RT = 16
CT = 64
SLOTS = 16
PER = 2
CHUNKS = SLOTS // PER
HALF = CHUNKS // 2
PIECES = 4
SPAN = CT * TS // (2 * PIECES)
GROUPS = 5
TICKS = GROUPS * HALF
NONE = 2 * GROUPS
FIRST = 7
MOST = 4
PLAN = (
    (2, 0, 9), (2, 1, 10), (2, -1, 11), (3, 0, 12), (3, 1, 13), (3, -1, 14),
    (4, 0, 15), (4, 1, 16), (4, -1, 16), (2, 2, 17), (2, -2, 17),
)
REST = (
    (3, 2), (3, -2), (2, 4), (2, 3), (2, -3), (4, 2), (4, -2),
    (3, 4), (3, 3), (3, -3), (4, 4), (4, 3), (4, -3),
)
MESH = pl.DeviceIdType.MESH


def rem(a, b):
    return lax.rem(a, jnp.int32(b))


def div(a, b):
    return lax.div(a, jnp.int32(b))


def kernel(
    tiles, rows_in, cols_in, live_in, dense, out,
    held, lists, lists_s, relay, both, split, acc, near, far, pair, done,
    local_sem,
    right_send, right_recv, left_send, left_recv, list_send, list_recv,
    hop1_send, hop1_recv, hop2_send, hop2_recv,
    near_send, near_recv, far_send, far_recv, pair_send, pair_recv, out_send, out_recv,
):
    row, col = lax.axis_index("row"), lax.axis_index("col")
    x_hi, z = div(row, NZ), rem(row, NZ)
    y, x_lo, core = div(col, 4), rem(div(col, 2), 2), rem(col, 2)
    x = x_hi * 2 + x_lo

    def device(x, y, z, core):
        return (div(x, 2) * NZ + z, y * 4 + rem(x, 2) * 2 + core)

    def copy(src, dst, send_sem, recv_sem, target):
        return pltpu.make_async_remote_copy(
            src_ref=src, dst_ref=dst, send_sem=send_sem, recv_sem=recv_sem,
            device_id=target, device_id_type=MESH,
        )

    up = device(x, y, rem(z + 1, NZ), core)
    down = device(x, y, rem(z + NZ - 1, NZ), core)
    forth = device(rem(x + 1, NX), y, z, core)
    back = device(rem(x + NX - 1, NX), y, z, core)

    barrier = pltpu.get_barrier_semaphore()
    partners = [device(x, y, rem(z + step, NZ), core) for step in range(1, NZ)]
    partners += [forth, back, device(x, y, z, 1 - core)]
    partners += [device(x, rem(y + step, NY), z, core) for step in (1, 2, 3)]
    for partner in partners:
        pl.semaphore_signal(barrier, inc=1, device_id=partner, device_id_type=MESH)

    center = col - x_hi * NZ

    def banded(source):
        gap = source - center
        return jnp.logical_and(gap >= -1, gap <= 1)

    crossed = jnp.logical_and(center >= -1, center <= NZ)

    def place(source):
        return rem(source - center + 3 + 4 * NZ, NZ) - 3

    def hops(source, half, way):
        u = place(source)
        first = jnp.where(u > 0, 4, 3)
        second = jnp.where(u < 0, 2, jnp.where(u > 0, 5, 4))
        even = 3 + rem(source, 2)
        rightwards = jnp.where(crossed, jnp.where(half == 1, second, first), even)
        return rightwards if way == 0 else NZ - 1 - rightwards

    def half_of(source, turn, way):
        swap = (place(source) >= 0) if way == 0 else (place(source) < 0)
        return rem(turn + jnp.where(swap, 1, 0), 2)

    def travels(source, half, level, way):
        there = jnp.logical_or(half == 0, banded(source))
        return jnp.logical_and(there, level < hops(source, half, way))

    def source_of(level, way):
        return rem(z + 2 * NZ + (-level - 1 if way == 0 else level + 1), NZ)

    own_groups = jnp.where(banded(z), 2, 1)
    coming, passed, onward = [], [], []
    for way in (0, 1):
        group = [jnp.int32(NONE)] * GROUPS
        count = jnp.int32(0)
        for g in range(2 * GROUPS):
            source = source_of(g // 2, way)
            there = travels(source, half_of(source, g % 2, way), g // 2, way)
            for n in range(GROUPS):
                group[n] = jnp.where(jnp.logical_and(there, count == n), g, group[n])
            count = count + jnp.where(there, 1, 0)
        coming.append(group)
        goes, slots = [], []
        slot = own_groups
        for n in range(GROUPS):
            level = div(group[n], 2)
            source = source_of(level, way)
            on = travels(source, half_of(source, rem(group[n], 2), way), level + 1, way)
            on = jnp.logical_and(on, group[n] < NONE)
            goes.append(jnp.where(on, 1, 0))
            slots.append(slot)
            slot = slot + goes[-1]
        passed.append(goes)
        onward.append(slots)

    def pick(values, n):
        chosen = values[0]
        for i in range(1, GROUPS):
            chosen = jnp.where(n == i, values[i], chosen)
        return chosen

    def ring_copy(source, j, slot, way):
        part = held.at[source, pl.ds(PER * j, PER)]
        if way == 0:
            return copy(part, part, right_send.at[slot], right_recv.at[slot], up)
        return copy(part, part, left_send.at[slot], left_recv.at[slot], down)

    def message(t, way):
        group = pick(coming[way], div(t, HALF))
        source = source_of(div(group, 2), way)
        j = half_of(source, rem(group, 2), way) * HALF + rem(t, HALF)
        return group < NONE, source, j

    def arrive(t, way):
        there, source, j = message(t, way)

        @pl.when(there)
        def _():
            ring_copy(source, j, t, way).wait_recv()
            n = div(t, HALF)

            @pl.when(pick(passed[way], n) == 1)
            def _():
                ring_copy(source, j, pick(onward[way], n) * HALF + rem(t, HALF), way).start()

    def own_message(k, way):
        turn = div(k, HALF)
        half = jnp.where(own_groups == 2, half_of(z, turn, way), 0)
        return turn < own_groups, ring_copy(z, half * HALF + rem(k, HALF), k, way)

    def ring_sent(k, way):
        made = ring_copy(z, 0, k, way)
        slot = div(k, HALF)
        count = own_groups
        for n in range(GROUPS):
            count = count + passed[way][n]
        pl.when(slot < count)(made.wait_send)

    def list_copy(p):
        peer = rem(z + p, NZ)
        return copy(lists.at[z], lists.at[z], list_send, list_recv, device(x, y, peer, core))

    seven = lists.at[pl.ds(0, NZ - 1)]
    all_lists = copy(seven, seven, list_send, list_recv, up)

    def columns(way, k):
        return pl.ds(pl.multiple_of((way * PIECES + k) * SPAN, SPAN), SPAN)

    def hop1(way, k):
        return copy(
            both.at[x_hi, :, columns(way, k)], relay.at[way, k],
            hop1_send.at[way], hop1_recv.at[way, k], (forth, back)[way],
        )

    def hop2(way, k, owner):
        return copy(
            relay.at[way, k], both.at[owner, :, columns(way, k)],
            hop2_send.at[way], hop2_recv.at[way], (forth, back)[way],
        )

    def all_pieces(way):
        part = both.at[1 - x_hi, :, pl.ds(way * PIECES * SPAN, PIECES * SPAN)]
        return (
            copy(part, part, hop1_send.at[way], hop2_recv.at[way], forth),
            copy(part, part, hop2_send.at[way], hop2_recv.at[way], forth),
        )

    def relayed(way):
        return div(rem(x + (NX - 1 if way == 0 else 1), NX), 2)

    own_lists = [
        pltpu.make_async_copy(ref, lists.at[z, k], local_sem.at[k])
        for k, ref in enumerate((rows_in, cols_in, live_in))
    ]

    own_tiles = pltpu.make_async_copy(tiles, held.at[z], local_sem.at[3])
    own_dense = pltpu.make_async_copy(dense, both.at[x_hi], local_sem.at[4])
    for made in own_lists:
        made.start()
    own_tiles.start()
    own_dense.start()

    for made in own_lists:
        made.wait()
    own_tiles.wait()
    pl.semaphore_wait(barrier, len(partners))

    @pl.loop(1, NZ)
    def _(p):
        list_copy(p).start()

    @pl.loop(0, CHUNKS)
    def _(k):
        for way in (0, 1):
            there, made = own_message(k, way)
            pl.when(there)(made.start)

    own_dense.wait()

    @pl.loop(0, PIECES)
    def _(k):
        for way in (0, 1):
            hop1(way, k).start()

    @pl.loop(0, NZ * RT)
    def _(i):
        acc[div(i, RT), rem(i, RT)] = jnp.zeros((2 * SHARE, TS), jnp.float32)

    def one_tile(b, slot):
        tile = held[b, slot]
        high = tile.astype(jnp.bfloat16)
        low = (tile - high.astype(jnp.float32)).astype(jnp.bfloat16)
        chosen = split[lists_s[b, 1, 0, slot]]
        dims = (((1,), (1,)), ((), ()))
        by_high = lax.dot_general(chosen, high, dims, preferred_element_type=jnp.float32)
        by_low = lax.dot_general(
            chosen[: 2 * SHARE], low, dims, preferred_element_type=jnp.float32
        )
        return by_high[: 2 * SHARE] + (by_high[2 * SHARE :] + by_low)

    def multiply(b, j):
        products = [one_tile(b, PER * j + s) for s in range(PER)]
        for k in range(RT):
            term = acc[b, k]
            for s in range(PER):
                slot = PER * j + s
                live = lists_s[b, 2, 0, slot].astype(jnp.float32)
                weight = jnp.where(lists_s[b, 0, 0, slot] == k, live, 0.0)
                term = term + weight * products[s]
            acc[b, k] = term

    def do_work(w, carry):
        @pl.when(w < 0)
        def _():
            for s in range(2):
                j = 2 * (w + HALF) + s
                pl.when(j < own_groups * HALF)(lambda: multiply(z, j))

        @pl.when(w >= 0)
        def _():
            for way in (0, 1):
                there, source, j = message(w, way)
                pl.when(there)(lambda: multiply(source, j))

        for i, when in ((0, -1), (1, 2 * HALF - 1), (-1, 2 * HALF - 1), (2, 4 * HALF - 1), (-2, 4 * HALF - 1)):
            pl.when(w == when)(lambda: near_copy(block(i)).start())
        return carry

    def block(i):
        return rem(z + i + NZ, NZ)

    def near_copy(b):
        return copy(
            acc.at[b, pl.ds((1 - core) * 8, 8)], near.at[b],
            near_send, near_recv.at[b], device(x, y, z, 1 - core),
        )

    def far_copy(b, step):
        there = rem(y + step, NY)
        return copy(
            acc.at[b, pl.ds(core * 8 + there * 2, 2)], far.at[b, step - 1],
            far_send, far_recv.at[b], device(x, there, z, core),
        )

    def pair_copy(b):
        return copy(
            acc.at[b, core * 8 + y * 2 + (1 - x_lo)], pair.at[b],
            pair_send, pair_recv.at[b], device(x_hi * 2 + 1 - x_lo, y, z, core),
        )

    mine = core * 8 + y * 2 + x_lo

    def out_copy(b, a):
        return copy(
            done.at[b, pl.ds(a * SHARE, SHARE)], out.at[:, pl.ds(pl.multiple_of(mine * TS, TS), TS)],
            out_send, out_recv, (x_hi * NZ + b, a * NZ + z),
        )

    def stage2(i):
        b = block(i)
        near_copy(b).wait_recv()

        @pl.loop(0, 8)
        def _(k):
            acc[b, core * 8 + k] = acc[b, core * 8 + k] + near[b, k]

        for step in (1, 2, 3):
            far_copy(b, step).start()

    def stage3(i):
        b = block(i)
        copy(far.at[b], far.at[b], far_send, far_recv.at[b], up).wait_recv()
        for k in range(2):
            place = core * 8 + y * 2 + k
            acc[b, place] = acc[b, place] + (far[b, 0, k] + far[b, 1, k] + far[b, 2, k])
        pair_copy(b).start()

    def is_home(b, a):
        return jnp.logical_and(b == z, a * NZ + z == col)

    def stage4(i):
        b = block(i)
        pair_copy(b).wait_recv()
        done[b] = acc[b, mine] + pair[b]
        for a in range(2):
            home = is_home(b, a)

            @pl.when(home)
            def _():
                out[:, pl.ds(pl.multiple_of(mine * TS, TS), TS)] = done[b, a * SHARE : (a + 1) * SHARE]

            @pl.when(jnp.logical_not(home))
            def _():
                out_copy(b, a).start()

    def prepare():
        all_lists.wait_recv()
        to_scalar = pltpu.make_async_copy(lists, lists_s, local_sem.at[0])
        to_scalar.start()
        for way in (0, 1):
            all_pieces(way)[1].wait_recv()

        @pl.loop(0, CT)
        def _(t):
            place = pl.ds(pl.multiple_of(t * TS, TS), TS)
            for a in range(2):
                value = both[a, :, place]
                high = value.astype(jnp.bfloat16)
                low = (value - high.astype(jnp.float32)).astype(jnp.bfloat16)
                split[t, a * SHARE : (a + 1) * SHARE] = high
                split[t, (2 + a) * SHARE : (3 + a) * SHARE] = low

        to_scalar.wait()

    def tick(t, worked):
        @pl.when(t < PIECES)
        def _():
            for way in (0, 1):
                hop1(way, t).wait_recv()
                hop2(way, t, relayed(way)).start()

        for way in (0, 1):
            arrive(t, way)
        pl.when(t == FIRST)(prepare)
        for stage, i, when in PLAN:
            pl.when(t == when)(lambda: (stage2, stage3, stage4)[stage - 2](i))
        stop = jnp.where(t < FIRST, worked, jnp.minimum(worked + MOST, t + 1))
        lax.fori_loop(worked, stop, do_work, 0)
        return stop

    lax.fori_loop(0, TICKS, tick, jnp.int32(-HALF))
    for i in (4, 3, -3):
        near_copy(block(i)).start()
    for stage, i in REST:
        (stage2, stage3, stage4)[stage - 2](i)

    homes = rem(col, NZ) == z

    @pl.when(homes)
    def _():
        part = out.at[:, pl.ds(0, (RT - 1) * TS)]
        copy(part, part, out_send, out_recv, up).wait()

    @pl.when(jnp.logical_not(homes))
    def _():
        copy(out, out, out_send, out_recv, up).wait()

    all_lists.wait_send()

    @pl.loop(0, TICKS)
    def _(k):
        for way in (0, 1):
            ring_sent(k, way)

    for way in (0, 1):
        for made in all_pieces(way):
            made.wait_send()
    copy(near, near, near_send, near_recv.at[0], up).wait_send()
    copy(far, far, far_send, far_recv.at[0], up).wait_send()
    copy(pair, pair, pair_send, pair_recv.at[0], up).wait_send()


def body(tile_values, tile_rows, tile_cols, tile_live, dense_factor):
    dma = pltpu.SemaphoreType.DMA
    vmem = pltpu.VMEM
    f32 = jnp.float32
    return pl.pallas_call(
        kernel,
        out_shape=jax.ShapeDtypeStruct((SHARE, RT * TS), f32),
        in_specs=[pl.BlockSpec(memory_space=pltpu.HBM)] * 5,
        out_specs=pl.BlockSpec(memory_space=pltpu.VMEM),
        scratch_shapes=[
            vmem((NZ, SLOTS, TS, TS), f32),
            vmem((NZ, 3, 1, SLOTS), jnp.int32),
            pltpu.SMEM((NZ, 3, 1, SLOTS), jnp.int32),
            vmem((2, PIECES, SHARE, SPAN), f32),
            vmem((2, SHARE, CT * TS), f32),
            vmem((CT, 4 * SHARE, TS), jnp.bfloat16),
            vmem((NZ, RT, 2 * SHARE, TS), f32),
            vmem((NZ, 8, 2 * SHARE, TS), f32),
            vmem((NZ, 3, 2, 2 * SHARE, TS), f32),
            vmem((NZ, 2 * SHARE, TS), f32),
            vmem((NZ, 2 * SHARE, TS), f32),
            dma((5,)),
            dma((TICKS,)), dma((TICKS,)), dma((TICKS,)), dma((TICKS,)),
            dma, dma,
            dma((2,)), dma((2, PIECES)), dma((2,)), dma((2,)),
            dma, dma((NZ,)), dma, dma((NZ,)), dma, dma((NZ,)), dma, dma,
        ],
        compiler_params=pltpu.CompilerParams(
            collective_id=0, has_side_effects=True, vmem_limit_bytes=67043328
        ),
    )(tile_values[0, 0], tile_rows[0], tile_cols[0], tile_live[0], dense_factor)


def solution(mesh):
    in_specs = (
        P("row", "col", None, None, None),
        P("row", "col", None),
        P("row", "col", None),
        P("row", "col", None),
        P("row", "col"),
    )
    out_specs = P("col", "row")
    return jax.shard_map(body, mesh=mesh, in_specs=in_specs, out_specs=out_specs, check_vma=False)
```

time: 218 us -> 92.1 us (0.42); the launches traced: 215 us -> 92 us
  waiting for transfers between devices: 99.8 us -> 0 us
  Pallas kernels: 0 us -> 90.3 us
  blocking collectives: 56.1 us -> 0 us
  starting transfers between devices: 18 us -> 0 us
  matrix products: 15.7 us -> 0 us
  local copies, waits for them, and re-layouts: 14.9 us -> 1.67 us
  other arithmetic: 11.1 us -> 0 us
    all_to_all x2 -> x0, waiting for transfers between devices: 99.8 us -> none  [the longest x1 93.7 us: body(): lax.all_to_all(outgoing, 'row', split_axis=1, concat_axis=0, tiled=True)]
    pallas_call x0 -> x1, Pallas kernels: none -> 90.3 us  [body(): pl.pallas_call(kernel, out_shape=jax.ShapeDtypeStruct((SHARE, RT * TS), f...]
    all_to_all x1 -> x0, blocking collectives: 56.1 us -> none  [sum_at_owner(): lax.all_to_all(in_blocks(value, dim, length), axis, 0, 0, tiled=True)]
    all_to_all x2 -> x0, starting transfers between devices: 18 us -> none  [the longest x1 10.9 us: from_everyone(): lax.all_to_all(jnp.broadcast_to(value[None], (length, *value.shape)), axi...]
    dot_general x2 -> x0, matrix products: 15.7 us -> none  [the longest x1 9.41 us: tile_product(): jnp.einsum('wsk,sik->wsi', selected, masked, precision=lax.Precision.HIGH...]
    select_n x2 -> x0, other arithmetic: 7.92 us -> none  [body(): jnp.take(dense_factor.reshape(width_share, CT, tile_size), wanted, axis=1)]
    transpose x1 -> x0, local copies, waits for them, and re-layouts: 5.45 us -> none  [tile_product(): jnp.einsum('wsk,sik->wsi', selected, masked, precision=lax.Precision.HIGH...]
    another operation x1 -> x0, local copies, waits for them, and re-layouts: 4.87 us -> none  [in_blocks(): return jnp.moveaxis(value.reshape(*before, length, -1, *after), dim, 0)]
  transfers between devices with their start and end apart: 2 -> 0, of which waited for: 2 -> 0; matrix products, arithmetic and copies ran while one was open for 0% -> 0% of each run, Pallas kernels for 0% -> 0%
where the time goes in v4:
time: 92.1 us; the launch traced here: 92 us
  Pallas kernels  90.3 us (98%)
  local copies, waits for them, and re-layouts  1.67 us (2%)
    pallas_call x1, Pallas kernels, body(): pl.pallas_call(kernel, out_shape=jax.ShapeDtypeStruct((SHARE, RT * TS), f...  90.3 us

profile of v4, /device:TPU:7, one launch (start us, length us, event | category | flops | bytes accessed | tf_op | source)
XLA Modules:
  0.0 92.0 jit_solution(2866418437002704026)
XLA Ops:
  0.0 90.3 %shard_map.55 = f32[32,2048]{1,0:T(8,128)} custom-call(f32[16,128,128]{2,1,0:T(8,128)} %bitcast.4, s32[1,16]{1,0:T(1,128)} %bitcast.5, s32[1,16]{1,0:T(1,128)} %bitcast.6, s32[1,16]{1,0:T(1,128)} %bitcast.7, f32[32,8192]{1,0:T(8,128)} %dense.1), custom_call_target="tpu_custom_call" | custom-call | tf_op jit(solution)/shard_map/pallas_call | solution.py:423
  90.3 1.7 %copy.7 = f32[32,2048]{1,0:T(8,128)} copy(f32[32,2048]{1,0:T(8,128)} %shard_map.55) | data formatting | bytes 524288

commit v5 on v4

--- a/solution.py
+++ b/solution.py
@@ -23,11 +23,7 @@
 MOST = 4
 PLAN = (
     (2, 0, 9), (2, 1, 10), (2, -1, 11), (3, 0, 12), (3, 1, 13), (3, -1, 14),
-    (4, 0, 15), (4, 1, 16), (4, -1, 16), (2, 2, 17), (2, -2, 17),
-)
-REST = (
-    (3, 2), (3, -2), (2, 4), (2, 3), (2, -3), (4, 2), (4, -2),
-    (3, 4), (3, 3), (3, -3), (4, 4), (4, 3), (4, -3),
+    (4, 0, 15), (2, 2, 16), (2, -2, 16), (4, 1, 16), (4, -1, 17), (3, 2, 18),
 )
 MESH = pl.DeviceIdType.MESH
 
@@ -42,11 +38,12 @@
 
 def kernel(
     tiles, rows_in, cols_in, live_in, dense, out,
-    held, lists, lists_s, relay, both, split, acc, near, far, pair, done,
+    held, lists, lists_s, relay, both, split, acc, near, far, pair, done, across, beside, landing,
     local_sem,
     right_send, right_recv, left_send, left_recv, list_send, list_recv,
     hop1_send, hop1_recv, hop2_send, hop2_recv,
     near_send, near_recv, far_send, far_recv, pair_send, pair_recv, out_send, out_recv,
+    across_send, across_recv, beside_send, beside_recv, halves_send,
 ):
     row, col = lax.axis_index("row"), lax.axis_index("col")
     x_hi, z = div(row, NZ), rem(row, NZ)
@@ -240,7 +237,9 @@
 
     @pl.loop(0, NZ * RT)
     def _(i):
-        acc[div(i, RT), rem(i, RT)] = jnp.zeros((2 * SHARE, TS), jnp.float32)
+        acc[div(i, RT), div(rem(i, RT), 8), div(rem(i, 8), 2), rem(i, 2)] = jnp.zeros(
+            (2 * SHARE, TS), jnp.float32
+        )
 
     def one_tile(b, slot):
         tile = held[b, slot]
@@ -257,13 +256,14 @@
     def multiply(b, j):
         products = [one_tile(b, PER * j + s) for s in range(PER)]
         for k in range(RT):
-            term = acc[b, k]
+            place_of = (b, k // 8, k // 2 % NY, k % 2)
+            term = acc[place_of]
             for s in range(PER):
                 slot = PER * j + s
                 live = lists_s[b, 2, 0, slot].astype(jnp.float32)
                 weight = jnp.where(lists_s[b, 0, 0, slot] == k, live, 0.0)
                 term = term + weight * products[s]
-            acc[b, k] = term
+            acc[place_of] = term
 
     def do_work(w, carry):
         @pl.when(w < 0)
@@ -287,67 +287,114 @@
 
     def near_copy(b):
         return copy(
-            acc.at[b, pl.ds((1 - core) * 8, 8)], near.at[b],
+            acc.at[b, 1 - core], near.at[b],
             near_send, near_recv.at[b], device(x, y, z, 1 - core),
         )
 
     def far_copy(b, step):
         there = rem(y + step, NY)
         return copy(
-            acc.at[b, pl.ds(core * 8 + there * 2, 2)], far.at[b, step - 1],
+            acc.at[b, core, there], far.at[b, step - 1],
             far_send, far_recv.at[b], device(x, there, z, core),
         )
 
+    neighbour = device(x_hi * 2 + 1 - x_lo, y, z, core)
+
     def pair_copy(b):
-        return copy(
-            acc.at[b, core * 8 + y * 2 + (1 - x_lo)], pair.at[b],
-            pair_send, pair_recv.at[b], device(x_hi * 2 + 1 - x_lo, y, z, core),
-        )
-
-    mine = core * 8 + y * 2 + x_lo
+        return copy(acc.at[b, core, y, 1 - x_lo], pair.at[b], pair_send, pair_recv.at[b], neighbour)
+
+    def tile_row(k):
+        return pl.ds(pl.multiple_of((core * 8 + y * 2 + k) * TS, TS), TS)
 
     def out_copy(b, a):
         return copy(
-            done.at[b, pl.ds(a * SHARE, SHARE)], out.at[:, pl.ds(pl.multiple_of(mine * TS, TS), TS)],
+            done.at[b, pl.ds(a * SHARE, SHARE)], landing.at[0, :, tile_row(x_lo)],
             out_send, out_recv, (x_hi * NZ + b, a * NZ + z),
         )
 
-    def stage2(i):
-        b = block(i)
+    def is_home(b, a):
+        return jnp.logical_and(b == z, a * NZ + z == col)
+
+    def go_home(b):
+        for a in range(2):
+            home = is_home(b, a)
+
+            @pl.when(home)
+            def _():
+                landing[0, :, tile_row(x_lo)] = done[b, a * SHARE : (a + 1) * SHARE]
+
+            pl.when(jnp.logical_not(home))(out_copy(b, a).start)
+
+    def take_near(b):
         near_copy(b).wait_recv()
 
         @pl.loop(0, 8)
         def _(k):
-            acc[b, core * 8 + k] = acc[b, core * 8 + k] + near[b, k]
-
+            spot = (b, core, div(k, 2), rem(k, 2))
+            acc[spot] = acc[spot] + near[b, div(k, 2), rem(k, 2)]
+
+    def take_far(b):
+        copy(far.at[b], far.at[b], far_send, far_recv.at[b], up).wait_recv()
+        for k in range(2):
+            spot = (b, core, y, k)
+            acc[spot] = acc[spot] + (far[b, 0, k] + far[b, 1, k] + far[b, 2, k])
+
+    def stage2(i):
+        b = block(i)
+        take_near(b)
         for step in (1, 2, 3):
             far_copy(b, step).start()
 
     def stage3(i):
         b = block(i)
-        copy(far.at[b], far.at[b], far_send, far_recv.at[b], up).wait_recv()
+        take_far(b)
+        pair_copy(b).start()
+
+    def stage4(i):
+        b = block(i)
+        pair_copy(b).wait_recv()
+        done[b] = acc[b, core, y, x_lo] + pair[b]
+        go_home(b)
+
+    def stage3_home(i):
+        b = block(i)
+        take_far(b)
         for k in range(2):
-            place = core * 8 + y * 2 + k
-            acc[b, place] = acc[b, place] + (far[b, 0, k] + far[b, 1, k] + far[b, 2, k])
-        pair_copy(b).start()
-
-    def is_home(b, a):
-        return jnp.logical_and(b == z, a * NZ + z == col)
-
-    def stage4(i):
-        b = block(i)
-        pair_copy(b).wait_recv()
-        done[b] = acc[b, mine] + pair[b]
-        for a in range(2):
-            home = is_home(b, a)
-
-            @pl.when(home)
-            def _():
-                out[:, pl.ds(pl.multiple_of(mine * TS, TS), TS)] = done[b, a * SHARE : (a + 1) * SHARE]
-
-            @pl.when(jnp.logical_not(home))
-            def _():
-                out_copy(b, a).start()
+            for a in range(2):
+                copy(
+                    acc.at[b, core, y, k, pl.ds(a * SHARE, SHARE)], landing.at[x_lo, :, tile_row(k)],
+                    halves_send, out_recv, (x_hi * NZ + b, a * NZ + z),
+                ).start()
+
+    def across_copy(b):
+        return copy(acc.at[b, core, :, 1 - x_lo], across, across_send, across_recv, neighbour)
+
+    def beside_copy(b, step):
+        there = rem(y + step, NY)
+        return copy(
+            acc.at[b, core, there, x_lo], beside.at[step - 1],
+            beside_send, beside_recv, device(x, there, z, core),
+        )
+
+    def stage2_across(i):
+        b = block(i)
+        take_near(b)
+        across_copy(b).start()
+
+    def stage3_across(i):
+        b = block(i)
+        across_copy(b).wait_recv()
+        for k in range(NY):
+            spot = (b, core, k, x_lo)
+            acc[spot] = acc[spot] + across[k]
+        for step in (1, 2, 3):
+            beside_copy(b, step).start()
+
+    def stage4_across(i):
+        b = block(i)
+        copy(beside, beside, beside_send, beside_recv, up).wait_recv()
+        done[b] = acc[b, core, y, x_lo] + (beside[0] + beside[1] + beside[2])
+        go_home(b)
 
     def prepare():
         all_lists.wait_recv()
@@ -387,20 +434,22 @@
     lax.fori_loop(0, TICKS, tick, jnp.int32(-HALF))
     for i in (4, 3, -3):
         near_copy(block(i)).start()
-    for stage, i in REST:
-        (stage2, stage3, stage4)[stage - 2](i)
-
-    homes = rem(col, NZ) == z
-
-    @pl.when(homes)
-    def _():
-        part = out.at[:, pl.ds(0, (RT - 1) * TS)]
-        copy(part, part, out_send, out_recv, up).wait()
-
-    @pl.when(jnp.logical_not(homes))
-    def _():
-        copy(out, out, out_send, out_recv, up).wait()
-
+    stage3(-2)
+    stage4(2)
+    stage2(4)
+    stage2_across(3)
+    stage2(-3)
+    stage4(-2)
+    stage3(4)
+    stage3_across(3)
+    stage4(4)
+    stage3_home(-3)
+    stage4_across(3)
+
+    part = landing.at[0, :, pl.ds(0, 4 * TS)]
+    copy(part, part, halves_send, out_recv, up).wait_send()
+    across_copy(0).wait_send()
+    copy(beside, beside, beside_send, beside_recv, up).wait_send()
     all_lists.wait_send()
 
     @pl.loop(0, TICKS)
@@ -412,8 +461,39 @@
         for made in all_pieces(way):
             made.wait_send()
     copy(near, near, near_send, near_recv.at[0], up).wait_send()
-    copy(far, far, far_send, far_recv.at[0], up).wait_send()
-    copy(pair, pair, pair_send, pair_recv.at[0], up).wait_send()
+    part = far.at[pl.ds(0, NZ - 1)]
+    copy(part, part, far_send, far_recv.at[0], up).wait_send()
+    part = pair.at[pl.ds(0, NZ - 2)]
+    copy(part, part, pair_send, pair_recv.at[0], up).wait_send()
+
+    way_home = rem(z - rem(col, NZ) + NZ, NZ)
+    halved = way_home == NZ - 3
+    homes = way_home == 0
+
+    @pl.when(halved)
+    def _():
+        copy(landing, landing, out_send, out_recv, up).wait_recv()
+        out[...] = landing[0] + landing[1]
+
+    @pl.when(homes)
+    def _():
+        part = landing.at[0, :, pl.ds(0, (RT - 1) * TS)]
+        copy(part, part, out_send, out_recv, up).wait_recv()
+        part = landing.at[0, :, pl.ds(0, 13 * TS)]
+        copy(part, part, out_send, out_recv, up).wait_send()
+
+    @pl.when(jnp.logical_not(homes))
+    def _():
+        part = landing.at[0, :, pl.ds(0, 14 * TS)]
+        copy(part, part, out_send, out_recv, up).wait_send()
+
+    @pl.when(jnp.logical_not(jnp.logical_or(halved, homes)))
+    def _():
+        copy(landing.at[0], landing.at[0], out_send, out_recv, up).wait_recv()
+
+    @pl.when(jnp.logical_not(halved))
+    def _():
+        out[...] = landing[0]
 
 
 def body(tile_values, tile_rows, tile_cols, tile_live, dense_factor):
@@ -432,16 +512,20 @@
             vmem((2, PIECES, SHARE, SPAN), f32),
             vmem((2, SHARE, CT * TS), f32),
             vmem((CT, 4 * SHARE, TS), jnp.bfloat16),
-            vmem((NZ, RT, 2 * SHARE, TS), f32),
-            vmem((NZ, 8, 2 * SHARE, TS), f32),
+            vmem((NZ, 2, NY, 2, 2 * SHARE, TS), f32),
+            vmem((NZ, NY, 2, 2 * SHARE, TS), f32),
             vmem((NZ, 3, 2, 2 * SHARE, TS), f32),
             vmem((NZ, 2 * SHARE, TS), f32),
             vmem((NZ, 2 * SHARE, TS), f32),
+            vmem((NY, 2 * SHARE, TS), f32),
+            vmem((3, 2 * SHARE, TS), f32),
+            vmem((2, SHARE, RT * TS), f32),
             dma((5,)),
             dma((TICKS,)), dma((TICKS,)), dma((TICKS,)), dma((TICKS,)),
             dma, dma,
             dma((2,)), dma((2, PIECES)), dma((2,)), dma((2,)),
             dma, dma((NZ,)), dma, dma((NZ,)), dma, dma((NZ,)), dma, dma,
+            dma, dma, dma, dma, dma,
         ],
         compiler_params=pltpu.CompilerParams(
             collective_id=0, has_side_effects=True, vmem_limit_bytes=67043328

time: 92.1 us -> 89.3 us (0.970)
  Pallas kernels: 90.3 us -> 87.5 us
    pallas_call x1, Pallas kernels: 90.3 us -> 87.5 us  [body(): pl.pallas_call(kernel, out_shape=jax.ShapeDtypeStruct((SHARE, RT * TS), f...]
where the time goes in v5:
time: 89.3 us; the launch traced here: 89.1 us
  Pallas kernels  87.5 us (98%)
  local copies, waits for them, and re-layouts  1.67 us (2%)
    pallas_call x1, Pallas kernels, body(): pl.pallas_call(kernel, out_shape=jax.ShapeDtypeStruct((SHARE, RT * TS), f...  87.5 us

profile of v5, /device:TPU:7, one launch (start us, length us, event | category | flops | bytes accessed | tf_op | source)
XLA Modules:
  0.0 89.1 jit_solution(8553845626862940479)
XLA Ops:
  0.0 87.5 %shard_map.55 = f32[32,2048]{1,0:T(8,128)} custom-call(f32[16,128,128]{2,1,0:T(8,128)} %bitcast.4, s32[1,16]{1,0:T(1,128)} %bitcast.5, s32[1,16]{1,0:T(1,128)} %bitcast.6, s32[1,16]{1,0:T(1,128)} %bitcast.7, f32[32,8192]{1,0:T(8,128)} %dense.1), custom_call_target="tpu_custom_call" | custom-call | tf_op jit(solution)/shard_map/pallas_call | solution.py:503
  87.5 1.7 %copy.7 = f32[32,2048]{1,0:T(8,128)} copy(f32[32,2048]{1,0:T(8,128)} %shard_map.55) | data formatting | bytes 524288

commit v6 on v5

--- a/solution.py
+++ b/solution.py
@@ -23,7 +23,7 @@
 MOST = 4
 PLAN = (
     (2, 0, 9), (2, 1, 10), (2, -1, 11), (3, 0, 12), (3, 1, 13), (3, -1, 14),
-    (4, 0, 15), (2, 2, 16), (2, -2, 16), (4, 1, 16), (4, -1, 17), (3, 2, 18),
+    (4, 0, 15), (2, 2, 16), (2, -2, 16), (4, 1, 16), (4, -1, 17),
 )
 MESH = pl.DeviceIdType.MESH
 
@@ -77,6 +77,7 @@
         gap = source - center
         return jnp.logical_and(gap >= -1, gap <= 1)
 
+    both_of = jnp.logical_and
     crossed = jnp.logical_and(center >= -1, center <= NZ)
 
     def place(source):
@@ -135,8 +136,8 @@
     def ring_copy(source, j, slot, way):
         part = held.at[source, pl.ds(PER * j, PER)]
         if way == 0:
-            return copy(part, part, right_send.at[slot], right_recv.at[slot], up)
-        return copy(part, part, left_send.at[slot], left_recv.at[slot], down)
+            return copy(part, part, right_send, right_recv.at[slot], up)
+        return copy(part, part, left_send, left_recv.at[slot], down)
 
     def message(t, way):
         group = pick(coming[way], div(t, HALF))
@@ -161,13 +162,14 @@
         half = jnp.where(own_groups == 2, half_of(z, turn, way), 0)
         return turn < own_groups, ring_copy(z, half * HALF + rem(k, HALF), k, way)
 
-    def ring_sent(k, way):
-        made = ring_copy(z, 0, k, way)
-        slot = div(k, HALF)
+    def ring_sent(way):
         count = own_groups
         for n in range(GROUPS):
             count = count + passed[way][n]
-        pl.when(slot < count)(made.wait_send)
+        for c in range(1, GROUPS + 1):
+            part = held.at[pl.ds(0, c), pl.ds(0, PER * HALF)]
+            sem = right_send if way == 0 else left_send
+            pl.when(count == c)(copy(part, part, sem, right_recv.at[0], up).wait_send)
 
     def list_copy(p):
         peer = rem(z + p, NZ)
@@ -253,30 +255,31 @@
         )
         return by_high[: 2 * SHARE] + (by_high[2 * SHARE :] + by_low)
 
-    def multiply(b, j):
-        products = [one_tile(b, PER * j + s) for s in range(PER)]
-        for k in range(RT):
-            place_of = (b, k // 8, k // 2 % NY, k % 2)
-            term = acc[place_of]
-            for s in range(PER):
-                slot = PER * j + s
-                live = lists_s[b, 2, 0, slot].astype(jnp.float32)
-                weight = jnp.where(lists_s[b, 0, 0, slot] == k, live, 0.0)
-                term = term + weight * products[s]
-            acc[place_of] = term
+    def multiply(*messages):
+        products = [[one_tile(b, PER * j + s) for s in range(PER)] for b, j in messages]
+        for (b, j), pair_of in zip(messages, products):
+            slots = [PER * j + s for s in range(PER)]
+            lives = [lists_s[b, 2, 0, slot].astype(jnp.float32) for slot in slots]
+            for k in range(RT):
+                place_of = (b, k // 8, k // 2 % NY, k % 2)
+                term = acc[place_of]
+                for s in range(PER):
+                    weight = jnp.where(lists_s[b, 0, 0, slots[s]] == k, lives[s], 0.0)
+                    term = term + weight * pair_of[s]
+                acc[place_of] = term
 
     def do_work(w, carry):
-        @pl.when(w < 0)
+        @pl.when(both_of(w < 0, 2 * (w + HALF) < own_groups * HALF))
         def _():
-            for s in range(2):
-                j = 2 * (w + HALF) + s
-                pl.when(j < own_groups * HALF)(lambda: multiply(z, j))
+            multiply((z, 2 * (w + HALF)), (z, 2 * (w + HALF) + 1))
 
         @pl.when(w >= 0)
         def _():
-            for way in (0, 1):
-                there, source, j = message(w, way)
-                pl.when(there)(lambda: multiply(source, j))
+            there, source, j = message(w, 0)
+            there_too, source_too, j_too = message(w, 1)
+            pl.when(both_of(there, there_too))(lambda: multiply((source, j), (source_too, j_too)))
+            alone, alone_j = jnp.where(there, source, source_too), jnp.where(there, j, j_too)
+            pl.when(there != there_too)(lambda: multiply((alone, alone_j)))
 
         for i, when in ((0, -1), (1, 2 * HALF - 1), (-1, 2 * HALF - 1), (2, 4 * HALF - 1), (-2, 4 * HALF - 1)):
             pl.when(w == when)(lambda: near_copy(block(i)).start())
@@ -434,11 +437,12 @@
     lax.fori_loop(0, TICKS, tick, jnp.int32(-HALF))
     for i in (4, 3, -3):
         near_copy(block(i)).start()
+    stage3(2)
     stage3(-2)
-    stage4(2)
     stage2(4)
     stage2_across(3)
     stage2(-3)
+    stage4(2)
     stage4(-2)
     stage3(4)
     stage3_across(3)
@@ -452,10 +456,8 @@
     copy(beside, beside, beside_send, beside_recv, up).wait_send()
     all_lists.wait_send()
 
-    @pl.loop(0, TICKS)
-    def _(k):
-        for way in (0, 1):
-            ring_sent(k, way)
+    for way in (0, 1):
+        ring_sent(way)
 
     for way in (0, 1):
         for made in all_pieces(way):
@@ -521,14 +523,14 @@
             vmem((3, 2 * SHARE, TS), f32),
             vmem((2, SHARE, RT * TS), f32),
             dma((5,)),
-            dma((TICKS,)), dma((TICKS,)), dma((TICKS,)), dma((TICKS,)),
+            dma, dma((TICKS,)), dma, dma((TICKS,)),
             dma, dma,
             dma((2,)), dma((2, PIECES)), dma((2,)), dma((2,)),
             dma, dma((NZ,)), dma, dma((NZ,)), dma, dma((NZ,)), dma, dma,
             dma, dma, dma, dma, dma,
         ],
         compiler_params=pltpu.CompilerParams(
-            collective_id=0, has_side_effects=True, vmem_limit_bytes=67043328
+            collective_id=0, has_side_effects=True, vmem_limit_bytes=56000000
         ),
     )(tile_values[0, 0], tile_rows[0], tile_cols[0], tile_live[0], dense_factor)
 

time: 89.3 us -> 87 us (0.974)
  Pallas kernels: 87.5 us -> 85 us
    pallas_call x1, Pallas kernels: 87.5 us -> 85 us  [body(): pl.pallas_call(kernel, out_shape=jax.ShapeDtypeStruct((SHARE, RT * TS), f...]
where the time goes in v6:
time: 87 us; the launch traced here: 86.4 us
  Pallas kernels  85 us (98%)
  local copies, waits for them, and re-layouts  1.39 us (2%)
    pallas_call x1, Pallas kernels, body(): pl.pallas_call(kernel, out_shape=jax.ShapeDtypeStruct((SHARE, RT * TS), f...  85 us

profile of v6, /device:TPU:7, one launch (start us, length us, event | category | flops | bytes accessed | tf_op | source)
XLA Modules:
  0.0 86.4 jit_solution(17584212591461231819)
XLA Ops:
  0.0 0.0 copy-start
  0.0 0.0 copy-start.1
  0.0 0.0 copy-start.2
  0.0 0.6 copy-done
  0.7 0.0 copy-done.1
  0.7 0.0 copy-done.2
  0.7 85.0 %shard_map.55 = f32[32,2048]{1,0:T(8,128)S(1)} custom-call(f32[16,128,128]{2,1,0:T(8,128)} %bitcast.7, s32[1,16]{1,0:T(1,128)S(1)} %bitcast.4, s32[1,16]{1,0:T(1,128)S(1)} %bitcast.5, s32[1,16]{1,0:T(1,128)S(1)} %bitcast.6, f32[32,8192]{1,0:T(8,128)} %dense.1), custom_call_target="tpu_custom_call" | custom-call | tf_op jit(solution)/shard_map/pallas_call | solution.py:505
  85.7 0.7 copy.7
Async XLA Ops:
  0.0 0.7 copy-start
  0.0 0.7 copy-start.1
  0.0 0.7 copy-start.2

commit v7 on v6

--- a/solution.py
+++ b/solution.py
@@ -19,11 +19,12 @@
 GROUPS = 5
 TICKS = GROUPS * HALF
 NONE = 2 * GROUPS
+LAST = 17
 FIRST = 7
 MOST = 4
 PLAN = (
     (2, 0, 9), (2, 1, 10), (2, -1, 11), (3, 0, 12), (3, 1, 13), (3, -1, 14),
-    (4, 0, 15), (2, 2, 16), (2, -2, 16), (4, 1, 16), (4, -1, 17),
+    (4, 0, 15), (4, 1, 16), (2, 2, 16), (2, -2, 17), (4, -1, 17),
 )
 MESH = pl.DeviceIdType.MESH
 
@@ -418,6 +419,18 @@
 
         to_scalar.wait()
 
+    low = center - core
+    early = jnp.logical_or(low < -2, low > NZ)
+
+    def last_near():
+        for i in (4, 3, -3):
+            near_copy(block(i)).start()
+
+    def last_stage2():
+        stage2(4)
+        stage2_across(3)
+        stage2(-3)
+
     def tick(t, worked):
         @pl.when(t < PIECES)
         def _():
@@ -430,18 +443,17 @@
         pl.when(t == FIRST)(prepare)
         for stage, i, when in PLAN:
             pl.when(t == when)(lambda: (stage2, stage3, stage4)[stage - 2](i))
+        pl.when(both_of(early, t == LAST))(last_near)
+        pl.when(both_of(early, t == LAST + 1))(last_stage2)
         stop = jnp.where(t < FIRST, worked, jnp.minimum(worked + MOST, t + 1))
         lax.fori_loop(worked, stop, do_work, 0)
         return stop
 
     lax.fori_loop(0, TICKS, tick, jnp.int32(-HALF))
-    for i in (4, 3, -3):
-        near_copy(block(i)).start()
+    pl.when(jnp.logical_not(early))(last_near)
     stage3(2)
     stage3(-2)
-    stage2(4)
-    stage2_across(3)
-    stage2(-3)
+    pl.when(jnp.logical_not(early))(last_stage2)
     stage4(2)
     stage4(-2)
     stage3(4)

time: 87 us -> 86.7 us (level)
  no operation moved by 1% of the time
where the time goes in v7:
time: 86.7 us; the launch traced here: 86.1 us
  Pallas kernels  84.7 us (98%)
  local copies, waits for them, and re-layouts  1.39 us (2%)
    pallas_call x1, Pallas kernels, body(): pl.pallas_call(kernel, out_shape=jax.ShapeDtypeStruct((SHARE, RT * TS), f...  84.7 us

profile of v7, /device:TPU:7, one launch (start us, length us, event | category | flops | bytes accessed | tf_op | source)
XLA Modules:
  0.0 86.1 jit_solution(2918387076916759810)
XLA Ops:
  0.0 0.0 copy-start
  0.0 0.0 copy-start.1
  0.0 0.0 copy-start.2
  0.0 0.6 copy-done
  0.7 0.0 copy-done.1
  0.7 0.0 copy-done.2
  0.7 84.7 %shard_map.55 = f32[32,2048]{1,0:T(8,128)S(1)} custom-call(f32[16,128,128]{2,1,0:T(8,128)} %bitcast.7, s32[1,16]{1,0:T(1,128)S(1)} %bitcast.4, s32[1,16]{1,0:T(1,128)S(1)} %bitcast.5, s32[1,16]{1,0:T(1,128)S(1)} %bitcast.6, f32[32,8192]{1,0:T(8,128)} %dense.1), custom_call_target="tpu_custom_call" | custom-call | tf_op jit(solution)/shard_map/pallas_call | solution.py:517
  85.4 0.7 copy.7
Async XLA Ops:
  0.0 0.7 copy-start
  0.0 0.7 copy-start.1
  0.0 0.7 copy-start.2

commit v8 on v7

--- a/solution.py
+++ b/solution.py
@@ -544,7 +544,12 @@
         compiler_params=pltpu.CompilerParams(
             collective_id=0, has_side_effects=True, vmem_limit_bytes=56000000
         ),
-    )(tile_values[0, 0], tile_rows[0], tile_cols[0], tile_live[0], dense_factor)
+    )(
+        *(
+            pltpu.with_memory_space_constraint(value, pltpu.HBM)
+            for value in (tile_values[0, 0], tile_rows[0], tile_cols[0], tile_live[0], dense_factor)
+        )
+    )
 
 
 def solution(mesh):

time: 86.7 us -> 86 us (level)
  no operation moved by 1% of the time
where the time goes in v8:
time: 86 us; the launch traced here: 85.4 us
  Pallas kernels  84.7 us (98%)
    pallas_call x1, Pallas kernels, body(): pl.pallas_call(kernel, out_shape=jax.ShapeDtypeStruct((SHARE, RT * TS), f...  84.7 us

profile of v8, /device:TPU:7, one launch (start us, length us, event | category | flops | bytes accessed | tf_op | source)
XLA Modules:
  0.0 85.4 jit_solution(8916724180437280845)
XLA Ops:
  0.0 84.7 %shard_map.55 = f32[32,2048]{1,0:T(8,128)S(1)} custom-call(f32[16,128,128]{2,1,0:T(8,128)} %bitcast.4, s32[1,16]{1,0:T(1,128)} %bitcast.5, s32[1,16]{1,0:T(1,128)} %bitcast.6, s32[1,16]{1,0:T(1,128)} %bitcast.7, f32[32,8192]{1,0:T(8,128)} %dense.1), custom_call_target="tpu_custom_call" | custom-call | tf_op jit(solution)/shard_map/pallas_call | solution.py:517
  84.7 0.7 copy.7

commit v9 on v8

--- a/solution.py
+++ b/solution.py
@@ -20,6 +20,7 @@
 TICKS = GROUPS * HALF
 NONE = 2 * GROUPS
 LAST = 17
+EARLY = 4
 FIRST = 7
 MOST = 4
 PLAN = (
@@ -40,7 +41,7 @@
 def kernel(
     tiles, rows_in, cols_in, live_in, dense, out,
     held, lists, lists_s, relay, both, split, acc, near, far, pair, done, across, beside, landing,
-    local_sem,
+    word, local_sem,
     right_send, right_recv, left_send, left_recv, list_send, list_recv,
     hop1_send, hop1_recv, hop2_send, hop2_recv,
     near_send, near_recv, far_send, far_recv, pair_send, pair_recv, out_send, out_recv,
@@ -66,8 +67,7 @@
     back = device(rem(x + NX - 1, NX), y, z, core)
 
     barrier = pltpu.get_barrier_semaphore()
-    partners = [device(x, y, rem(z + step, NZ), core) for step in range(1, NZ)]
-    partners += [forth, back, device(x, y, z, 1 - core)]
+    partners = [up, down, forth, back, device(x, y, z, 1 - core)]
     partners += [device(x, rem(y + step, NY), z, core) for step in (1, 2, 3)]
     for partner in partners:
         pl.semaphore_signal(barrier, inc=1, device_id=partner, device_id_type=MESH)
@@ -221,22 +221,33 @@
     own_tiles.wait()
     pl.semaphore_wait(barrier, len(partners))
 
-    @pl.loop(1, NZ)
-    def _(p):
-        list_copy(p).start()
-
-    @pl.loop(0, CHUNKS)
-    def _(k):
+    def own_start(k):
         for way in (0, 1):
             there, made = own_message(k, way)
             pl.when(there)(made.start)
 
+    for k in range(EARLY):
+        own_start(k)
     own_dense.wait()
 
     @pl.loop(0, PIECES)
     def _(k):
         for way in (0, 1):
             hop1(way, k).start()
+
+    for step in range(NZ // 2 - 1):
+        for side, target in enumerate((up, down)):
+            pl.semaphore_signal(word.at[step, side], inc=1, device_id=target, device_id_type=MESH)
+        for side in (0, 1):
+            pl.semaphore_wait(word.at[step, side], 1)
+
+    @pl.loop(1, NZ)
+    def _(p):
+        list_copy(p).start()
+
+    @pl.loop(EARLY, CHUNKS)
+    def _(k):
+        own_start(k)
 
     @pl.loop(0, NZ * RT)
     def _(i):
@@ -534,6 +545,7 @@
             vmem((NY, 2 * SHARE, TS), f32),
             vmem((3, 2 * SHARE, TS), f32),
             vmem((2, SHARE, RT * TS), f32),
+            pltpu.SemaphoreType.REGULAR((NZ // 2 - 1, 2)),
             dma((5,)),
             dma, dma((TICKS,)), dma, dma((TICKS,)),
             dma, dma,

time: 86 us -> 86.4 us (level)
  no operation moved by 1% of the time
where the time goes in v9:
time: 86.4 us; the launch traced here: 86.2 us
  Pallas kernels  85.5 us (99%)
    pallas_call x1, Pallas kernels, body(): pl.pallas_call(kernel, out_shape=jax.ShapeDtypeStruct((SHARE, RT * TS), f...  85.5 us

profile of v9, /device:TPU:7, one launch (start us, length us, event | category | flops | bytes accessed | tf_op | source)
XLA Modules:
  0.0 86.2 jit_solution(18116277100749784336)
XLA Ops:
  0.0 85.5 %shard_map.55 = f32[32,2048]{1,0:T(8,128)S(1)} custom-call(f32[16,128,128]{2,1,0:T(8,128)} %bitcast.4, s32[1,16]{1,0:T(1,128)} %bitcast.5, s32[1,16]{1,0:T(1,128)} %bitcast.6, s32[1,16]{1,0:T(1,128)} %bitcast.7, f32[32,8192]{1,0:T(8,128)} %dense.1), custom_call_target="tpu_custom_call" | custom-call | tf_op jit(solution)/shard_map/pallas_call | solution.py:528
  85.5 0.7 copy.7
